TPU v7x, 256 devices: a 2x2x32 block of a 4x8x32 slice. The times are simulated.
256 devices in a mesh: member: 4 (over x, y), lon: 32 (over z), lat: 2 (over core).
Axes of the slice: x: 2, y: 2, z: 32, core: 2. Of those that a mesh axis runs over, the one named last changes fastest.
The devices are a block of a 4x8x32 slice.
Arguments:
- strain_rate: float32 [3, 1024, 2160], P(None, 'lon', 'lat'), may hold values from -6 to 6
- stress_start: float32 [3, 1024, 2160], P(None, 'lon', 'lat'), may hold values from -3 to 3
- concentration: float32 [1024, 2160], P('lon', 'lat'), may hold values from 0.5 to 1
- cell_class: int32 [4096, 2160], P(('member', 'lon'), 'lat'), parts along dimension 0, may hold values from 0 to 7
- land_mask: int32 [1024, 2160], P('lon', 'lat'), may hold values 0 or 1
- fold_partner: int32 [1024], replicated, may hold values from 0 to 1023, each once
- kernel_weights: float32 [7, 7], replicated, may hold values from 0.05 to 0.5
Outputs:
- stress_out: float32 [3, 4096, 2160], P(None, ('member', 'lon'), 'lat'), parts along dimension 1
- damage_out: float32 [4096, 2160], P(('member', 'lon'), 'lat'), parts along dimension 0
- mean_overstress: float32 [12], P('member'), parts along dimension 0
There are 4 independent parts, one for each index of `member`. A program takes and returns all parts, laid end to end along the dimension named above; an argument that names none is the same for every part. Nothing has to cross between parts.
Inputs may be any that keep to these rules, and one draw needn't show every extreme that they name: `fold_partner`: each of the 1024 longitude indices appears once.
All inputs are finite; a program needn't handle non-finite values. No bound on the sum of `land_mask` on one device may be relied on, other than what follows from the above.
Results may differ from a plain program's by a relative error of at most 0.0001.
Values sent between devices are 32-bit elements; how exact they have to be, the bound alone decides.
No kernel may reach another device: no remote copies, remote signals or barrier semaphores. Data moves between devices by JAX's collectives and lax.ppermute only.
A program may use at most 64 MiB of HBM per device.

v0:
```python
import jax
import jax.numpy as jnp
from jax import lax
from jax.sharding import PartitionSpec as P

ITERS = 3


def joined_along(tiles, dim):
    shape = list(tiles.shape[1:])
    shape[dim] *= tiles.shape[0]
    return jnp.moveaxis(tiles, 0, dim).reshape(shape)


def copy_for_each(array, axis):
    copies = jnp.broadcast_to(array, (lax.axis_size(axis), *array.shape))
    return lax.all_to_all(copies, axis, split_axis=0, concat_axis=0, tiled=True)


def collect(array, axis, dim):
    return joined_along(copy_for_each(array, axis), dim)


def padded_2(array, sides, width, wrap):
    for axis, dim in sides:
        size, length = (lax.axis_size(axis), array.shape[dim])
        up = [(i, (i + 1) % size) for i in range(size if wrap else size - 1)]
        down = [(j, i) for i, j in up]
        last = lax.slice_in_dim(array, length - width, length, axis=dim)
        first = lax.slice_in_dim(array, 0, width, axis=dim)
        before = lax.ppermute(last, axis, up)
        after = lax.ppermute(first, axis, down)
        array = jnp.concatenate([before, array, after], axis=dim)
    return array


def over_copies(array, axis):
    return copy_for_each(array, axis).sum(axis=0)


def in_one(arrays, axis):
    flat, at, gathered = (jnp.concatenate([a.reshape(-1) for a in arrays]), 0, [])
    so_far = over_copies(flat, axis)
    for a in arrays:
        gathered.append(so_far[at : at + a.size].reshape(a.shape))
        at += a.size
    return tuple(gathered)


def smooth(padded, weights, ncols, nrows):
    side = weights.shape[0]
    total = jnp.zeros((padded.shape[0], ncols, nrows), jnp.float32)
    for first in range(side):
        for second in range(side):
            total = (
                total
                + weights[first, second] * padded[:, first : first + ncols, second : second + nrows]
            )
    return total


def extend(fields, partner, width):
    ncols = fields.shape[1]
    top = jnp.swapaxes(fields[:, :, -width:], 1, 2)
    whole_top = collect(top, "lon", 2)
    total_cols = whole_top.shape[2]
    first_col = lax.axis_index("lon") * ncols
    columns = (first_col - width + jnp.arange(ncols + 2 * width, dtype=jnp.int32)) % total_cols
    picked = jnp.take(partner, columns)
    rows = jnp.take(whole_top, picked, axis=2)
    north = jnp.swapaxes(rows[:, ::-1, :], 1, 2)
    lat_place = lax.axis_index("lat")
    lat_last = lax.axis_size("lat") - 1
    wide = padded_2(fields, (("lon", 1),), width, True)
    padded = padded_2(wide, (("lat", 2),), width, False)
    south_rim = padded[:, :, :width]
    north_rim = jnp.where(lat_place == lat_last, north, padded[:, :, -width:])
    return jnp.concatenate([south_rim, padded[:, :, width:-width], north_rim], axis=2)


def ocean_excess(local_excess, count):
    excess, ocean_total = in_one((local_excess, count), ("lon", "lat"))
    return excess / (ocean_total + 1.0)


def shards(
    strain_rate, stress_start, concentration, cell_class, land_mask, fold_partner, kernel_weights
):
    width = kernel_weights.shape[0] // 2
    ocean = land_mask.astype(jnp.float32)
    ncols, nrows = ocean.shape
    denom = smooth(extend(ocean[None], fold_partner, width), kernel_weights, ncols, nrows)[0] + 1.0
    count = jnp.sum(ocean)
    damage = ocean * 0.1 * cell_class.astype(jnp.float32) * concentration
    stress = ocean[None] * stress_start
    base = concentration * jnp.exp(-2.0 * (1.0 - concentration))
    e_one, e_two, e_shear = (strain_rate[0], strain_rate[1], strain_rate[2])
    load = jnp.stack([e_one + e_two / 3.0, e_two + e_one / 3.0, e_shear / (4.0 / 3.0)]) / (
        8.0 / 9.0
    )
    means = []
    for step in range(ITERS):
        keep = 1.0 - damage
        theta = 0.5 / (keep * keep)
        elastic = ocean[None] * (stress + (base * keep)[None] * load) / (1.0 + theta)[None]
        half_diff = (elastic[0] - elastic[1]) / 2.0
        tau = jnp.sqrt(half_diff * half_diff + elastic[2] * elastic[2] + 0.25)
        ratio = (tau + 0.7 * (elastic[0] + elastic[1]) / 2.0) / (0.6 * concentration)
        over = jnp.maximum(ratio, 1.0)
        q_part = 1.0 - 1.0 / over
        local_excess = jnp.sum(ocean * (over - 1.0))
        mean_now = ocean_excess(local_excess, count)
        factor = 1.0 / (1.0 + 2.0 * mean_now)
        local_damage = ocean * (damage + factor * keep * q_part)
        local_stress = elastic * (1.0 - factor * q_part)[None]
        fields = jnp.concatenate([local_damage[None], local_stress], axis=0)
        averaged = (
            smooth(extend(fields, fold_partner, width), kernel_weights, ncols, nrows) / denom[None]
        )
        fresh = ocean[None] * (0.5 * fields + 0.5 * averaged)
        means.append(mean_now)
        damage = fresh[0]
        stress = fresh[1:]
    return (stress, damage, jnp.stack(means))


def solution(mesh):
    in_specs = (
        P(None, "lon", "lat"),
        P(None, "lon", "lat"),
        P("lon", "lat"),
        P(("member", "lon"), "lat"),
        P("lon", "lat"),
        P(),
        P(),
    )
    out_specs = (P(None, ("member", "lon"), "lat"), P(("member", "lon"), "lat"), P("member"))
    return jax.shard_map(shards, mesh=mesh, in_specs=in_specs, out_specs=out_specs, check_vma=False)
```

profile of v0, /device:TPU:38, one launch (start us, length us, event | category | flops | bytes accessed | tf_op | source)
XLA Modules:
  0.0 419.3 jit_solution(5917433452330927474)
XLA Ops:
  0.7 1.0 convert_bitcast_fusion
  1.7 1.1 multiply_add_fusion.1
  2.8 1.8 multiply_multiply_fusion.2
  5.5 1.4 pad_maximum_fusion.28
  7.5 34.2 %all-to-all-start = ((f32[64,1,2]{2,1,0:T(1,128)}), f32[64,1,2]{2,1,0:T(1,128)S(1)}, u32[]{:S(2)}, u32[]{:S(2)}) async-start(f32[64,1,2]{2,1,0:T(1,128)} %broadcast_in_dim.79), calls=%async_computation | async-start | bytes 65536 | tf_op jit(solution)/shard_map/all_to_all | solution.py:17
  41.7 2.9 collective-permute-start.5
  47.8 15.9 %all-to-all-done = f32[64,1,2]{2,1,0:T(1,128)S(1)} async-done(((f32[64,1,2]{2,1,0:T(1,128)}), f32[64,1,2]{2,1,0:T(1,128)S(1)}, u32[]{:S(2)}, u32[]{:S(2)}) %all-to-all-start) | async-done | bytes 544 | tf_op jit(solution)/shard_map/all_to_all | solution.py:17
  64.3 5.0 %all-to-all-start.2 = ((f32[32,1,3,32]{3,1,2,0:T(1,128)}), f32[32,1,3,32]{3,1,2,0:T(1,128)S(1)}, u32[]{:S(2)}, u32[]{:S(2)}) async-start(f32[32,1,3,32]{3,1,2,0:T(1,128)} %broadcast_in_dim.84), calls=%async_computation.2 | async-start | bytes 98304 | tf_op jit(solution)/shard_map/all_to_all | solution.py:17
  71.5 2.9 collective-permute-start.1
  74.5 0.8 reshape.237
  75.4 1.3 collective-permute-start.6
  76.7 1.3 collective-permute-start.7
  78.0 2.4 collective-permute-done
  81.1 1.9 collective-permute-start.2
  83.1 1.3 collective-permute-start.3
  84.5 8.5 %all-to-all-done.2 = f32[32,1,3,32]{3,1,2,0:T(1,128)S(1)} async-done(((f32[32,1,3,32]{3,1,2,0:T(1,128)}), f32[32,1,3,32]{3,1,2,0:T(1,128)S(1)}, u32[]{:S(2)}, u32[]{:S(2)}) %all-to-all-start.2) | async-done | bytes 12320 | tf_op jit(solution)/shard_map/all_to_all | solution.py:17
  93.0 12.9 %all-to-all-start.1 = ((f32[32,1,384]{2,1,0:T(1,128)}), f32[32,1,384]{2,1,0:T(1,128)S(1)}, u32[]{:S(2)}, u32[]{:S(2)}) async-start(f32[32,1,384]{2,1,0:T(1,128)} %reshape.237), calls=%async_computation.1 | async-start | bytes 98304 | tf_op jit(solution)/shard_map/all_to_all | solution.py:17
  105.9 1.1 copy.170
  107.0 1.6 gather_fusion
  109.6 32.4 %fusion.171 = f32[32,1080]{1,0:T(8,128)} fusion(f32[1,32,1080]{2,1,0:T(8,128)S(1)} %get-tuple-element.68, f32[1,3,1080]{2,1,0:T(4,128)S(1)} %collective-permute-done.5, f32[1,3,1080]{2,1,0:T(4,128)S(1)} %collective-permute-done.4, f32[1,38,1083]{2,1,0:T(8,128)S(1)} %get-tuple-element.59, f32[1,38,1083]{2,1,0:T(8,128)S(1)} %get-tuple-element.58, ...), kind=kLoop, calls=%fused_computation.370 | loop fusion | flops 3628800 | bytes 6246916 | tf_op jit(solution)/shard_map/div | solution.py:118
  143.4 1.9 copy.183
  145.3 2.3 gather_fusion.2
  147.9 0.9 bitcast_select_fusion.2
  148.8 1.2 maximum_maximum_fusion
  150.0 37.1 %fusion.105 = f32[4,32,1080]{2,1,0:T(8,128)S(1)} fusion(f32[4,38,1083]{2,1,0:T(8,128)S(1)} %get-tuple-element.38, f32[4,35,1080]{2,1,0:T(8,128)S(1)} %get-tuple-element.50, f32[4,38,1083]{2,1,0:T(8,128)S(1)} %get-tuple-element.37, f32[4,35,1080]{2,1,0:T(8,128)S(1)} %get-tuple-element.49, f32[3,32,1080]{2,1,0:T(8,128)S(1)} %broadcast_multiply_fusion.2, ...), kind=kLoop, calls=%fused_computation.240 | loop fusion | flops 13962240 | bytes 27924676 | tf_op jit(solution)/shard_map/mul | solution.py:120
  188.0 1.3 pad_maximum_fusion.29
  189.3 45.3 %all_to_all.38 = f32[64,1,2]{2,1,0:T(1,128)S(1)} all-to-all(f32[64,1,2]{2,1,0:T(1,128)S(1)} %broadcast_in_dim.87), channel_id=1, replica_groups=mesh['member'=4,'lon'=32,'lat'=2] {'lon','lat'}, dimensions={0} | all-to-all | bytes 1024 | tf_op jit(solution)/shard_map/all_to_all | solution.py:17
  237.3 1.5 collective-permute-start.8
  239.8 4.8 %all-to-all-start.4 = ((f32[32,1,384]{2,1,0:T(1,128)}), f32[32,1,384]{2,1,0:T(1,128)S(1)}, u32[]{:S(2)}, u32[]{:S(2)}) async-start(f32[32,1,384]{2,1,0:T(1,128)} %reshape.239), calls=%async_computation.4 | async-start | bytes 98304 | tf_op jit(solution)/shard_map/all_to_all | solution.py:17
  245.3 1.9 collective-permute-start.10
  247.2 1.5 collective-permute-start.11
  248.9 18.7 %all-to-all-done.4 = f32[32,1,384]{2,1,0:T(1,128)S(1)} async-done(((f32[32,1,384]{2,1,0:T(1,128)}), f32[32,1,384]{2,1,0:T(1,128)S(1)}, u32[]{:S(2)}, u32[]{:S(2)}) %all-to-all-start.4) | async-done | bytes 49184 | tf_op jit(solution)/shard_map/all_to_all | solution.py:17
  268.4 1.9 copy.185
  270.3 2.3 gather_fusion.3
  272.9 0.9 bitcast_select_fusion.1
  273.8 1.2 maximum_maximum_fusion.2
  275.0 37.1 %fusion.54 = f32[4,32,1080]{2,1,0:T(8,128)S(1)} fusion(f32[4,38,1083]{2,1,0:T(8,128)S(1)} %get-tuple-element.34, f32[4,35,1080]{2,1,0:T(8,128)S(1)} %get-tuple-element.46, f32[4,38,1083]{2,1,0:T(8,128)S(1)} %get-tuple-element.33, f32[4,35,1080]{2,1,0:T(8,128)S(1)} %get-tuple-element.45, f32[3,32,1080]{2,1,0:T(8,128)S(1)} %broadcast_multiply_fusion.1, ...), kind=kLoop, calls=%fused_computation.141 | loop fusion | flops 13962240 | bytes 27924676 | tf_op jit(solution)/shard_map/mul | solution.py:120
  313.0 1.3 pad_maximum_fusion.30
  314.3 27.7 %all_to_all.39 = f32[64,1,2]{2,1,0:T(1,128)S(1)} all-to-all(f32[64,1,2]{2,1,0:T(1,128)S(1)} %broadcast_in_dim.90), channel_id=1, replica_groups=mesh['member'=4,'lon'=32,'lat'=2] {'lon','lat'}, dimensions={0} | all-to-all | bytes 1024 | tf_op jit(solution)/shard_map/all_to_all | solution.py:17
  344.8 1.5 collective-permute-start.12
  347.8 4.8 %all-to-all-start.6 = ((f32[32,1,384]{2,1,0:T(1,128)}), f32[32,1,384]{2,1,0:T(1,128)S(1)}, u32[]{:S(2)}, u32[]{:S(2)}) async-start(f32[32,1,384]{2,1,0:T(1,128)} %reshape.241), calls=%async_computation.6 | async-start | bytes 98304 | tf_op jit(solution)/shard_map/all_to_all | solution.py:17
  352.7 1.3 collective-permute-start.14
  354.1 1.6 collective-permute-start.15
  355.7 20.1 %all-to-all-done.6 = f32[32,1,384]{2,1,0:T(1,128)S(1)} async-done(((f32[32,1,384]{2,1,0:T(1,128)}), f32[32,1,384]{2,1,0:T(1,128)S(1)}, u32[]{:S(2)}, u32[]{:S(2)}) %all-to-all-start.6) | async-done | bytes 49184 | tf_op jit(solution)/shard_map/all_to_all | solution.py:17
  376.7 1.9 copy.186
  378.7 2.3 gather_fusion.4
  381.6 36.2 %fusion.3 = f32[4,32,1080]{2,1,0:T(8,128)S(1)} fusion(f32[4,38,1083]{2,1,0:T(8,128)S(1)} %get-tuple-element.30, f32[4,35,1080]{2,1,0:T(8,128)S(1)} %get-tuple-element.42, f32[4,38,1083]{2,1,0:T(8,128)S(1)} %get-tuple-element.29, f32[4,35,1080]{2,1,0:T(8,128)S(1)} %get-tuple-element.41, f32[3,32,1080]{2,1,0:T(8,128)S(1)} %broadcast_multiply_fusion, ...), kind=kLoop, calls=%fused_computation.42 | loop fusion | flops 13962240 | bytes 27924676 | tf_op jit(solution)/shard_map/mul | solution.py:120
  417.8 0.8 slice.1726
  (124 shorter events, 21.0 us)
Async XLA Ops:
  0.6 46.3 %copy-start = (s32[1024]{0:T(1024)S(1)}, s32[1024]{0:T(1024)}, u32[]{:S(2)}) copy-start(s32[1024]{0:T(1024)} %param.16) | copy-start | bytes 12292
  0.6 4.1 copy-start.1
  0.7 4.1 copy-start.2
  0.7 4.0 copy-start.5
  2.8 41.9 %copy-start.7 = (f32[7,7]{1,0:T(8,128)S(1)}, f32[7,7]{1,0:T(8,128)}, u32[]{:S(2)}) copy-start(f32[7,7]{1,0:T(8,128)} %param.17) | copy-start | bytes 592
  2.8 68.4 %copy-start.6 = (s32[32,1080]{1,0:T(8,128)S(1)}, s32[32,1080]{1,0:T(8,128)}, u32[]{:S(2)}) copy-start(s32[32,1080]{1,0:T(8,128)} %param.14) | copy-start | bytes 414724
  7.5 56.2 %all-to-all-start = ((f32[64,1,2]{2,1,0:T(1,128)}), f32[64,1,2]{2,1,0:T(1,128)S(1)}, u32[]{:S(2)}, u32[]{:S(2)}) async-start(f32[64,1,2]{2,1,0:T(1,128)} %broadcast_in_dim.79), calls=%async_computation | async-start | bytes 65536 | tf_op jit(solution)/shard_map/all_to_all | solution.py:17
  41.7 33.6 %collective-permute-start.5 = (f32[1,3,1080]{2,1,0:T(4,128)S(1)}, f32[1,3,1080]{2,1,0:T(4,128)S(1)}, u32[]{:S(2)}, u32[]{:S(2)}) collective-permute-start(f32[1,3,1080]{2,1,0:T(4,128)S(1)} %get-tuple-element.67), channel_id=1, source_target_pairs={{2,0},{4,2},{6,4},{8,6},{10,8},{12,10},{14,12},{16,14},{18,16},{20... | collective-permute-start | bytes 38888 | tf_op jit(solution)/shard_map/ppermute | solution.py:32
  44.6 30.7 %collective-permute-start.4 = (f32[1,3,1080]{2,1,0:T(4,128)S(1)}, f32[1,3,1080]{2,1,0:T(4,128)S(1)}, u32[]{:S(2)}, u32[]{:S(2)}) collective-permute-start(f32[1,3,1080]{2,1,0:T(4,128)S(1)} %get-tuple-element.66), channel_id=1, source_target_pairs={{0,2},{2,4},{4,6},{6,8},{8,10},{10,12},{12,14},{14,16},{16,18},{18... | collective-permute-start | bytes 38888 | tf_op jit(solution)/shard_map/ppermute | solution.py:31
  47.7 60.9 %copy-start.8 = (pred[38]{0:T(512)(128)(4,1)}, pred[38]{0:T(512)(128)(4,1)S(1)}, u32[]{:S(2)}) copy-start(pred[38]{0:T(512)(128)(4,1)S(1)} %get-tuple-element.26) | copy-start | bytes 118
  47.7 59.3 %copy-start.10 = (s32[1024]{0:T(1024)}, s32[1024]{0:T(1024)S(1)}, u32[]{:S(2)}) copy-start(s32[1024]{0:T(1024)S(1)} %pad_clamp_fusion) | copy-start | bytes 12292
  64.3 28.6 %all-to-all-start.2 = ((f32[32,1,3,32]{3,1,2,0:T(1,128)}), f32[32,1,3,32]{3,1,2,0:T(1,128)S(1)}, u32[]{:S(2)}, u32[]{:S(2)}) async-start(f32[32,1,3,32]{3,1,2,0:T(1,128)} %broadcast_in_dim.84), calls=%async_computation.2 | async-start | bytes 98304 | tf_op jit(solution)/shard_map/all_to_all | solution.py:17
  71.5 6.5 %collective-permute-start.1 = (f32[4,3,1080]{2,1,0:T(4,128)S(1)}, f32[4,3,1080]{2,1,0:T(4,128)S(1)}, u32[]{:S(2)}, u32[]{:S(2)}) collective-permute-start(f32[4,3,1080]{2,1,0:T(4,128)S(1)} %get-tuple-element.52), channel_id=1, source_target_pairs={{2,0},{4,2},{6,4},{8,6},{10,8},{12,10},{14,12},{16,14},{18,16},{20... | collective-permute-start | bytes 155528 | tf_op jit(solution)/shard_map/ppermute | solution.py:32
  74.4 6.0 %collective-permute-start = (f32[4,3,1080]{2,1,0:T(4,128)S(1)}, f32[4,3,1080]{2,1,0:T(4,128)S(1)}, u32[]{:S(2)}, u32[]{:S(2)}) collective-permute-start(f32[4,3,1080]{2,1,0:T(4,128)S(1)} %get-tuple-element.51), channel_id=1, source_target_pairs={{0,2},{2,4},{4,6},{6,8},{8,10},{10,12},{12,14},{14,16},{16,18},{18... | collective-permute-start | bytes 155528 | tf_op jit(solution)/shard_map/ppermute | solution.py:31
  75.4 34.1 %collective-permute-start.6 = (f32[1,38,3]{2,1,0:T(8,128)S(1)}, f32[1,38,3]{2,1,0:T(8,128)S(1)}, u32[]{:S(2)}, u32[]{:S(2)}) collective-permute-start(f32[1,38,3]{2,1,0:T(8,128)S(1)} %get-tuple-element.60), channel_id=1, source_target_pairs={{0,1},{2,3},{4,5},{6,7},{8,9},{10,11},{12,13},{14,15},{16,17},{18,... | collective-permute-start | bytes 1376 | tf_op jit(solution)/shard_map/ppermute | solution.py:31
  76.7 32.1 %collective-permute-start.7 = (f32[1,38,3]{2,1,0:T(8,128)S(1)}, f32[1,38,3]{2,1,0:T(8,128)}, u32[]{:S(2)}, u32[]{:S(2)}) collective-permute-start(f32[1,38,3]{2,1,0:T(8,128)S(1)} %get-tuple-element.61), channel_id=1, source_target_pairs={{1,0},{3,2},{5,4},{7,6},{9,8},{11,10},{13,12},{15,14},{17,16},{19,... | collective-permute-start | bytes 1376 | tf_op jit(solution)/shard_map/ppermute | solution.py:32
  81.1 67.6 %collective-permute-start.2 = (f32[4,38,3]{2,1,0:T(8,128)}, f32[4,38,3]{2,1,0:T(8,128)}, u32[]{:S(2)}, u32[]{:S(2)}) collective-permute-start(f32[4,38,3]{2,1,0:T(8,128)} %get-tuple-element.39), channel_id=1, source_target_pairs={{0,1},{2,3},{4,5},{6,7},{8,9},{10,11},{12,13},{14,15},{16,17},{18,... | collective-permute-start | bytes 5480 | tf_op jit(solution)/shard_map/ppermute | solution.py:31
  83.1 64.8 %collective-permute-start.3 = (f32[4,38,3]{2,1,0:T(8,128)}, f32[4,38,3]{2,1,0:T(8,128)}, u32[]{:S(2)}, u32[]{:S(2)}) collective-permute-start(f32[4,38,3]{2,1,0:T(8,128)} %get-tuple-element.40), channel_id=1, source_target_pairs={{1,0},{3,2},{5,4},{7,6},{9,8},{11,10},{13,12},{15,14},{17,16},{19,... | collective-permute-start | bytes 5480 | tf_op jit(solution)/shard_map/ppermute | solution.py:32
  93.0 49.1 %all-to-all-start.1 = ((f32[32,1,384]{2,1,0:T(1,128)}), f32[32,1,384]{2,1,0:T(1,128)S(1)}, u32[]{:S(2)}, u32[]{:S(2)}) async-start(f32[32,1,384]{2,1,0:T(1,128)} %reshape.237), calls=%async_computation.1 | async-start | bytes 98304 | tf_op jit(solution)/shard_map/all_to_all | solution.py:17
  142.1 5.6 %copy-start.9 = (pred[38]{0:T(512)(128)(4,1)S(1)}, pred[38]{0:T(512)(128)(4,1)}, u32[]{:S(2)}) copy-start(pred[38]{0:T(512)(128)(4,1)} %copy-done.8) | copy-start | bytes 118
  236.8 7.8 %collective-permute-start.9 = (f32[4,3,1080]{2,1,0:T(4,128)S(1)}, f32[4,3,1080]{2,1,0:T(4,128)S(1)}, u32[]{:S(2)}, u32[]{:S(2)}) collective-permute-start(f32[4,3,1080]{2,1,0:T(4,128)S(1)} %get-tuple-element.48), channel_id=1, source_target_pairs={{2,0},{4,2},{6,4},{8,6},{10,8},{12,10},{14,12},{16,14},{18,16},{20... | collective-permute-start | bytes 155528 | tf_op jit(solution)/shard_map/ppermute | solution.py:32
  237.3 7.2 %collective-permute-start.8 = (f32[4,3,1080]{2,1,0:T(4,128)S(1)}, f32[4,3,1080]{2,1,0:T(4,128)S(1)}, u32[]{:S(2)}, u32[]{:S(2)}) collective-permute-start(f32[4,3,1080]{2,1,0:T(4,128)S(1)} %get-tuple-element.47), channel_id=1, source_target_pairs={{0,2},{2,4},{4,6},{6,8},{8,10},{10,12},{12,14},{14,16},{16,18},{18... | collective-permute-start | bytes 155528 | tf_op jit(solution)/shard_map/ppermute | solution.py:31
  239.8 27.8 %all-to-all-start.4 = ((f32[32,1,384]{2,1,0:T(1,128)}), f32[32,1,384]{2,1,0:T(1,128)S(1)}, u32[]{:S(2)}, u32[]{:S(2)}) async-start(f32[32,1,384]{2,1,0:T(1,128)} %reshape.239), calls=%async_computation.4 | async-start | bytes 98304 | tf_op jit(solution)/shard_map/all_to_all | solution.py:17
  245.3 28.4 %collective-permute-start.10 = (f32[4,38,3]{2,1,0:T(8,128)}, f32[4,38,3]{2,1,0:T(8,128)}, u32[]{:S(2)}, u32[]{:S(2)}) collective-permute-start(f32[4,38,3]{2,1,0:T(8,128)} %get-tuple-element.35), channel_id=1, source_target_pairs={{0,1},{2,3},{4,5},{6,7},{8,9},{10,11},{12,13},{14,15},{16,17},{18,... | collective-permute-start | bytes 5480 | tf_op jit(solution)/shard_map/ppermute | solution.py:31
  247.2 25.6 %collective-permute-start.11 = (f32[4,38,3]{2,1,0:T(8,128)}, f32[4,38,3]{2,1,0:T(8,128)}, u32[]{:S(2)}, u32[]{:S(2)}) collective-permute-start(f32[4,38,3]{2,1,0:T(8,128)} %get-tuple-element.36), channel_id=1, source_target_pairs={{1,0},{3,2},{5,4},{7,6},{9,8},{11,10},{13,12},{15,14},{17,16},{19,... | collective-permute-start | bytes 5480 | tf_op jit(solution)/shard_map/ppermute | solution.py:32
  344.2 8.4 %collective-permute-start.13 = (f32[4,3,1080]{2,1,0:T(4,128)S(1)}, f32[4,3,1080]{2,1,0:T(4,128)S(1)}, u32[]{:S(2)}, u32[]{:S(2)}) collective-permute-start(f32[4,3,1080]{2,1,0:T(4,128)S(1)} %get-tuple-element.44), channel_id=1, source_target_pairs={{2,0},{4,2},{6,4},{8,6},{10,8},{12,10},{14,12},{16,14},{18,16},{20... | collective-permute-start | bytes 155528 | tf_op jit(solution)/shard_map/ppermute | solution.py:32
  344.8 7.8 %collective-permute-start.12 = (f32[4,3,1080]{2,1,0:T(4,128)S(1)}, f32[4,3,1080]{2,1,0:T(4,128)S(1)}, u32[]{:S(2)}, u32[]{:S(2)}) collective-permute-start(f32[4,3,1080]{2,1,0:T(4,128)S(1)} %get-tuple-element.43), channel_id=1, source_target_pairs={{0,2},{2,4},{4,6},{6,8},{8,10},{10,12},{12,14},{14,16},{16,18},{18... | collective-permute-start | bytes 155528 | tf_op jit(solution)/shard_map/ppermute | solution.py:31
  347.8 28.0 %all-to-all-start.6 = ((f32[32,1,384]{2,1,0:T(1,128)}), f32[32,1,384]{2,1,0:T(1,128)S(1)}, u32[]{:S(2)}, u32[]{:S(2)}) async-start(f32[32,1,384]{2,1,0:T(1,128)} %reshape.241), calls=%async_computation.6 | async-start | bytes 98304 | tf_op jit(solution)/shard_map/all_to_all | solution.py:17
  352.7 28.4 %collective-permute-start.14 = (f32[4,38,3]{2,1,0:T(8,128)S(1)}, f32[4,38,3]{2,1,0:T(8,128)S(1)}, u32[]{:S(2)}, u32[]{:S(2)}) collective-permute-start(f32[4,38,3]{2,1,0:T(8,128)S(1)} %get-tuple-element.31), channel_id=1, source_target_pairs={{0,1},{2,3},{4,5},{6,7},{8,9},{10,11},{12,13},{14,15},{16,17},{18,... | collective-permute-start | bytes 5480 | tf_op jit(solution)/shard_map/ppermute | solution.py:31
  354.1 27.1 %collective-permute-start.15 = (f32[4,38,3]{2,1,0:T(8,128)S(1)}, f32[4,38,3]{2,1,0:T(8,128)S(1)}, u32[]{:S(2)}, u32[]{:S(2)}) collective-permute-start(f32[4,38,3]{2,1,0:T(8,128)S(1)} %get-tuple-element.32), channel_id=1, source_target_pairs={{1,0},{3,2},{5,4},{7,6},{9,8},{11,10},{13,12},{15,14},{17,16},{19,... | collective-permute-start | bytes 5480 | tf_op jit(solution)/shard_map/ppermute | solution.py:32
  376.7 4.9 %copy-start.3 = (f32[32,1080]{1,0:T(8,128)S(1)}, f32[32,1080]{1,0:T(8,128)}, u32[]{:S(2)}) copy-start(f32[32,1080]{1,0:T(8,128)} %fusion.171) | copy-start | bytes 414724
  376.7 4.9 %copy-start.4 = (f32[32,1080]{1,0:T(8,128)S(1)}, f32[32,1080]{1,0:T(8,128)}, u32[]{:S(2)}) copy-start(f32[32,1080]{1,0:T(8,128)} %get-tuple-element.70) | copy-start | bytes 414724
where the time goes:
time: 422 us; the launch traced here: 419 us
  other arithmetic  165 us (39%)
  starting transfers between devices  83.8 us (20%)
  blocking collectives  72.9 us (17%)
  waiting for transfers between devices  65.7 us (16%)
  local copies, waits for them, and re-layouts  27.1 us (6%)
  between operations  5.01 us (1%)
    mul x3, other arithmetic, shards(): fresh = ocean[None] * (0.5 * fields + 0.5 * averaged)  110 us
    all_to_all x2, blocking collectives, copy_for_each(): return lax.all_to_all(copies, axis, split_axis=0, concat_axis=0, tiled=True)  72.9 us
    all_to_all x5, waiting for transfers between devices, copy_for_each(): return lax.all_to_all(copies, axis, split_axis=0, concat_axis=0, tiled=True)  63.2 us
    all_to_all x5, starting transfers between devices, copy_for_each(): return lax.all_to_all(copies, axis, split_axis=0, concat_axis=0, tiled=True)  61.7 us
    div x1, other arithmetic, shards(): smooth(extend(fields, fold_partner, width), kernel_weights, ncols, nrows)  32.4 us
    ppermute x8, starting transfers between devices, padded_2(): after = lax.ppermute(first, axis, down)  12.6 us
    ppermute x8, starting transfers between devices, padded_2(): before = lax.ppermute(last, axis, up)  9.52 us
    gather x4, local copies, waits for them, and re-layouts, extend(): rows = jnp.take(whole_top, picked, axis=2)  8.61 us
  transfers between devices with their start and end apart: 21, of which 5 were waited for; matrix products, arithmetic and copies ran while one was open for 15% of the time, Pallas kernels for 0%

commit v1 on v0

v1 whole, which is shorter than its diff:
```python
import functools
import jax
import jax.numpy as jnp
from jax import lax
from jax.experimental import pallas as pl
from jax.experimental.pallas import tpu as pltpu
from jax.sharding import PartitionSpec as P

ITERS = 3
HALO = 9
LANES = 128
PAD = 16
F32 = jnp.float32
VM = pl.BlockSpec(memory_space=pltpu.VMEM)
SM = pl.BlockSpec(memory_space=pltpu.SMEM)


def cost(flops, size):
    return pl.CostEstimate(flops=flops, bytes_accessed=size, transcendentals=0)


def physics(damage, stress, bl, rc, oc):
    keep = 1.0 - damage
    k2 = keep * keep
    g = oc * (k2 / (k2 + 0.5))
    e = [g * (stress[k] + keep * bl[k]) for k in range(3)]
    half = (e[0] - e[1]) * 0.5
    tau = jnp.sqrt(half * half + e[2] * e[2] + 0.25)
    over = jnp.maximum((tau + 0.35 * (e[0] + e[1])) * rc, 1.0)
    q = oc * (1.0 - 1.0 / over)
    return e, q, oc * (over - 1.0)


def tops(tiles, single, extra, at):
    t = jnp.concatenate(tiles, axis=0).T
    rows = [t[at - k : at - k + 1, :] for k in range(3)]
    for one in (single, extra):
        if one is not None:
            parts = [one] + [pltpu.roll(one, k, 1) for k in (1, 2)] + [jnp.zeros_like(one)]
            rows.append(jnp.concatenate(parts, axis=0).T[at : at + 1, :])
    return rows


def total(x):
    return jnp.sum(jnp.sum(x, axis=0, keepdims=True), axis=1, keepdims=True)


def first_kernel(nrows, lat_ref, strain, stress, conc, cls, mask, f_ref, lat_out, chunk_ref, sum_ref):
    nt = f_ref.shape[1]
    ncols = conc.shape[0]
    excess = jnp.zeros((ncols, LANES), F32)
    count = jnp.zeros((ncols, LANES), F32)
    last = {}
    lane = lax.broadcasted_iota(jnp.int32, (ncols, LANES), 1)
    f_ref[:, nt - 1] = jnp.zeros((8, ncols, LANES), F32)
    for c in range(nt):
        w = min(LANES, nrows - c * LANES)
        sl = slice(c * LANES, c * LANES + w)
        con = conc[:, sl]
        base = con * jnp.exp(-2.0 * (1.0 - con))
        oc = mask[:, sl].astype(F32)
        e1, e2, e3 = (strain[k, :, sl] for k in range(3))
        third = 1.0 / 3.0
        bl = [base * ((e1 + e2 * third) * 1.125), base * ((e2 + e1 * third) * 1.125), base * (e3 * (0.75 * 1.125))]
        st = [oc * stress[k, :, sl] for k in range(3)]
        d = oc * 0.1 * cls[:, sl].astype(F32) * con
        for k in range(3):
            f_ref[k, c, :, 0:w] = bl[k]
            f_ref[3 + k, c, :, 0:w] = st[k]
        f_ref[6, c, :, 0:w] = oc * con
        f_ref[7, c, :, 0:w] = d
    for c in range(nt):
        bl = [f_ref[k, c] for k in range(3)]
        st = [f_ref[3 + k, c] for k in range(3)]
        mc = f_ref[6, c]
        d = f_ref[7, c]
        oc = jnp.where(mc > 0.0, 1.0, 0.0)
        rc = 1.0 / (0.6 * jnp.where(mc > 0.0, mc, 1.0))
        e, q, over = physics(d, st, bl, rc, oc)
        excess = excess + over
        count = count + oc
    at = nrows - 1 - (nt - 1) * LANES
    rows = tops([d, q, e[0], e[1]], e[2], oc, at)
    s = total(excess)
    n = total(count)
    lane1 = lax.broadcasted_iota(jnp.int32, (1, LANES), 1)
    sums = jnp.where(lane1 == 96, s, 0.0) + jnp.where(lane1 == 97, n, 0.0)
    for k, row in enumerate(rows):
        chunk_ref[k : k + 1, :] = row
    sum_ref[...] = jnp.broadcast_to(sums, sum_ref.shape)
    north = lat_ref[0] == lat_ref[1]
    for f in range(8):
        lat_out[f] = jnp.where(north, f_ref[f, 0], f_ref[f, nt - 1])


def second_kernel(nrows, lat_ref, f_ref, lat_in, chunk_ref, sum_ref, sum_in, t8_ref, low_ref, high_ref, send_ref):
    nt = f_ref.shape[1]
    ncols = f_ref.shape[2]
    edge = nrows - (nt - 1) * LANES
    lane = lax.broadcasted_iota(jnp.int32, (ncols, LANES), 1)
    north = lat_ref[0] == lat_ref[1]
    own = lane < edge
    keep = jnp.where(north, (lane >= LANES - HALO).astype(jnp.int32), ((lane >= edge) & (lane < edge + HALO)).astype(jnp.int32)) > 0
    for f in range(8):
        got = jnp.where(north, pltpu.roll(lat_in[f], (LANES - edge) % LANES, 1), pltpu.roll(lat_in[f], edge, 1))
        t8_ref[f] = jnp.where(own, f_ref[f, nt - 1], jnp.where(keep, got, 0.0))
    for f in range(8):
        for c in range(nt):
            at = t8_ref.at[f] if c == nt - 1 else f_ref.at[f, c]
            low_ref[f, c] = at[0:8]
            low_ref[8, c, f : f + 1] = at[8:9]
            high_ref[f, c] = at[ncols - 8 : ncols]
            high_ref[8, c, f : f + 1] = at[ncols - 9 : ncols - 8]
    s = sum_ref[0:1, :] + sum_in[0:1, :]
    chunk = [chunk_ref[k : k + 1, :] for k in range(5)]
    chunk[3] = chunk[3] + s
    block = jnp.concatenate(chunk, axis=0)
    for n in range(send_ref.shape[0]):
        send_ref[n] = block


def ghosts(got_ref, sel_ref, col_ref, per, fields):
    n = got_ref.shape[0] // per
    parts = []
    for r in range(per):
        m = got_ref[pl.ds(r, n, stride=per), :]
        h = m.astype(jnp.bfloat16)
        m = m - h.astype(F32)
        h2 = m.astype(jnp.bfloat16)
        h3 = (m - h2.astype(F32)).astype(jnp.bfloat16)
        parts.append(jnp.concatenate([h, h2, h3], axis=0))
    picked = jnp.dot(sel_ref[...], jnp.concatenate(parts, axis=1), preferred_element_type=F32)
    lane = lax.broadcasted_iota(jnp.int32, (sel_ref.shape[0], LANES), 1)
    col = col_ref[...] == (lane & 31)
    group = lane >> 5
    picked = [jnp.where(col, picked[:, r * LANES : (r + 1) * LANES], 0.0) for r in range(per)]
    out = []
    for f in range(fields):
        vals = []
        for k in range(3):
            row, g = (k, f) if f < 4 else (3 + f - 4, k)
            vals.append(jnp.sum(jnp.where(group == g, picked[row], 0.0), axis=1, keepdims=True))
        out.append(vals)
    return out


def smooth_into(w_ref, g_ref, acc_ref, nf, lo, hi):
    nt = g_ref.shape[1]
    lane = lax.broadcasted_iota(jnp.int32, (8, LANES), 1)

    def body(step, _):
        f = step // (hi - lo)
        row = (lo + step % (hi - lo)) * 8
        mid, rolled, out = {}, {}, {}
        for c in range(nt):
            x = [g_ref[f, c, pl.ds(row + a - 3, 8), :] for a in range(7)]
            for b in range(7):
                t = w_ref[0, b] * x[0]
                for a in range(1, 7):
                    t = t + w_ref[a, b] * x[a]
                if b == 3:
                    mid[c] = t
                else:
                    rolled[c, b] = pltpu.roll(t, (3 - b) % LANES, 1)
        for c in range(nt):
            t = mid[c]
            for b in range(3):
                t = t + jnp.where(lane < 3 - b, rolled[(c - 1) % nt, b], rolled[c, b])
            for b in range(4, 7):
                t = t + jnp.where(lane >= LANES - (b - 3), rolled[(c + 1) % nt, b], rolled[c, b])
            acc_ref[f, c, pl.ds(pl.multiple_of(row, 8), 8), :] = t
        return 0

    lax.fori_loop(0, nf * (hi - lo), body, 0)


def put_ghosts(lat_ref, g_ref, gh, factor, nrows, row0, nrow, with_ocean):
    nt = g_ref.shape[1]
    edge = nrows - (nt - 1) * LANES
    lane = lax.broadcasted_iota(jnp.int32, (nrow, LANES), 1)
    north = (lat_ref[0] == lat_ref[1]).astype(jnp.int32)
    vals = []
    d, q = gh[0], gh[1]
    vals.append([d[k] + factor * (1.0 - d[k]) * q[k] for k in range(3)])
    for m in range(3):
        vals.append([gh[2 + m][k] * (1.0 - factor * q[k]) for k in range(3)])
    if with_ocean:
        vals.append(gh[5])
    for f, v in enumerate(vals):
        t = g_ref[f, nt - 1, row0 : row0 + nrow, :]
        for k in range(3):
            t = jnp.where(lane == jnp.where(north > 0, edge + k, -1), v[k][0:nrow], t)
        g_ref[f, nt - 1, row0 : row0 + nrow, :] = t


def step_sums(chunk_ref, sum_ref, rows, excess):
    s = total(excess)
    lane1 = lax.broadcasted_iota(jnp.int32, (1, LANES), 1)
    sums = jnp.where(lane1 == 96, s, 0.0)
    rows[3] = rows[3] + sums
    for k, row in enumerate(rows):
        chunk_ref[k : k + 1, :] = row
    zero = jnp.zeros((1, LANES), F32)
    for k in range(4):
        sum_ref[k : k + 1, :] = sums if k == 3 else zero


def lane_value(row, at):
    lane1 = lax.broadcasted_iota(jnp.int32, row.shape, 1)
    return jnp.sum(jnp.where(lane1 == at, row, 0.0), axis=1, keepdims=True)


def finish(nrows, ncols, g_ref, acc_ref, stat_in, dyn_ref, chunk_ref, sum_ref, lo, hi):
    nt = g_ref.shape[1]
    edge = nrows - (nt - 1) * LANES
    lane = lax.broadcasted_iota(jnp.int32, (8, LANES), 1)
    excess = jnp.zeros((8, LANES), F32)
    for c in range(nt):

        def body(i, excess):
            at = pl.ds(pl.multiple_of(i * 8, 8), 8)
            to = pl.ds(pl.multiple_of((i - lo) * 8, 8), 8)
            bl, rc, r = stat_in(c, at, to)
            new = [0.5 * g_ref[f, c, at, :] + r * acc_ref[f, c, at, :] for f in range(4)]
            oc = jnp.where(r > 0.0, 1.0, 0.0)
            e, q, over = physics(new[0], new[1:], bl, rc, oc)
            dyn_ref[0, c, to, :] = new[0]
            dyn_ref[1, c, to, :] = q
            for k in range(3):
                dyn_ref[2 + k, c, to, :] = e[k]
            mine = jnp.where((i >= PAD // 8) & (i < (PAD + ncols) // 8), over, 0.0)
            if c == nt - 1:
                mine = jnp.where(lane < edge, mine, 0.0)
            return excess + mine

        excess = lax.fori_loop(lo, hi, body, excess)
    own = slice(PAD - lo * 8, PAD - lo * 8 + ncols)
    tile = [dyn_ref[f, nt - 1, own, :] for f in range(5)]
    rows = tops(tile[:4], tile[4], None, edge - 1)
    step_sums(chunk_ref, sum_ref, rows, excess)


def third_kernel(
    nrows, lat_ref, w_ref, f_ref, t8_ref, low_in, high_in, got_ref, sel_ref, col_ref,
    dyn_ref, stat_ref, chunk_ref, sum_ref, mean_ref, g_ref, acc_ref, rc_ref,
):
    nt = f_ref.shape[1]
    ncols = f_ref.shape[2]
    rows = g_ref.shape[2]
    n = got_ref.shape[0] // 5
    sums = jnp.sum(got_ref[pl.ds(3, n, stride=5), :], axis=0, keepdims=True)
    count = lane_value(sums, 97) + 1.0
    mean = lane_value(sums, 96) / count
    factor = 1.0 / (1.0 + 2.0 * mean)
    lane1 = lax.broadcasted_iota(jnp.int32, (1, LANES), 1)
    mean_ref[...] = jnp.broadcast_to(jnp.where(lane1 == 0, mean, count), mean_ref.shape)
    factor8 = jnp.broadcast_to(factor, (8, LANES))
    lo, hi = 1, rows // 8 - 1
    for c in range(nt):

        def local(vals, row, nr, c=c):
            bl, st, mc, d = vals[0:3], vals[3:6], vals[6], vals[7]
            oc = jnp.where(mc > 0.0, 1.0, 0.0)
            rc = 1.0 / (0.6 * jnp.where(mc > 0.0, mc, 1.0))
            e, q, _ = physics(d, st, bl, rc, oc)
            f8 = factor8[0:nr]
            at = slice(row, row + nr)
            g_ref[0, c, at, :] = d + f8 * (1.0 - d) * q
            for k in range(3):
                g_ref[1 + k, c, at, :] = e[k] * (1.0 - f8 * q)
            g_ref[4, c, at, :] = oc
            if nr == 8:
                stat = slice(row - lo * 8, row - lo * 8 + 8)
                for k in range(3):
                    stat_ref[k, c, stat, :] = bl[k]
                stat_ref[3, c, stat, :] = rc

        local([high_in[8, c, f : f + 1, :] for f in range(8)], PAD - 9, 1)
        local([high_in[f, c] for f in range(8)], PAD - 8, 8)
        for i in range(ncols // 8):
            local([(t8_ref[f, 8 * i : 8 * i + 8, :] if c == nt - 1 else f_ref[f, c, 8 * i : 8 * i + 8, :]) for f in range(8)], PAD + 8 * i, 8)
        local([low_in[f, c] for f in range(8)], PAD + ncols, 8)
        local([low_in[8, c, f : f + 1, :] for f in range(8)], PAD + ncols + 8, 1)
    gh = ghosts(got_ref, sel_ref, col_ref, 5, 6)
    for i in range(lo, hi):
        stat_ref[4, nt - 1, 8 * (i - lo) : 8 * (i - lo) + 8, :] = g_ref[4, nt - 1, 8 * i : 8 * i + 8, :]
    put_ghosts(lat_ref, g_ref, gh, factor, nrows, 0, rows, True)
    smooth_into(w_ref, g_ref, acc_ref, 5, lo, hi)

    def stat_in(c, at, to):
        oc = stat_ref[4, c, to, :] if c == nt - 1 else g_ref[4, c, at, :]
        r = 0.5 * oc / (acc_ref[4, c, at, :] + 1.0)
        stat_ref[4, c, to, :] = r
        return [stat_ref[k, c, to, :] for k in range(3)], stat_ref[3, c, to, :], r

    finish(nrows, ncols, g_ref, acc_ref, stat_in, dyn_ref, chunk_ref, sum_ref, lo, hi)


def load_local(nrows, lat_ref, dyn_in, got_ref, sel_ref, col_ref, mean_in, mean_ref, g_ref):
    nt = g_ref.shape[1]
    n = got_ref.shape[0] // 4
    sums = jnp.sum(got_ref[pl.ds(3, n, stride=4), :], axis=0, keepdims=True)
    count = lane_value(mean_in[0:1, :], 1)
    mean = lane_value(sums, 96) / count
    factor = 1.0 / (1.0 + 2.0 * mean)
    lane1 = lax.broadcasted_iota(jnp.int32, (1, LANES), 1)
    mean_ref[...] = jnp.broadcast_to(jnp.where(lane1 == 0, mean, count), mean_ref.shape)
    f8 = jnp.broadcast_to(factor, (8, LANES))
    for c in range(nt):

        def body(i, _, c=c):
            fr = pl.ds(pl.multiple_of(i * 8, 8), 8)
            to = pl.ds(pl.multiple_of(i * 8 + 8, 8), 8)
            d, q = dyn_in[0, c, fr, :], dyn_in[1, c, fr, :]
            g_ref[0, c, to, :] = d + f8 * (1.0 - d) * q
            down = 1.0 - f8 * q
            for k in range(3):
                g_ref[1 + k, c, to, :] = dyn_in[2 + k, c, fr, :] * down
            return 0

        lax.fori_loop(0, dyn_in.shape[2] // 8, body, 0)
    gh = ghosts(got_ref, sel_ref, col_ref, 4, 5)
    put_ghosts(lat_ref, g_ref, gh, factor, nrows, 0, g_ref.shape[2], False)


def fourth_kernel(
    nrows, ncols, lat_ref, w_ref, dyn_in, stat_in_ref, got_ref, sel_ref, col_ref, mean_in,
    dyn_ref, chunk_ref, sum_ref, mean_ref, g_ref, acc_ref,
):
    load_local(nrows, lat_ref, dyn_in, got_ref, sel_ref, col_ref, mean_in, mean_ref, g_ref)
    lo, hi = 1, g_ref.shape[2] // 8 - 1
    smooth_into(w_ref, g_ref, acc_ref, 4, lo, hi)

    def stat_in(c, at, to):
        return [stat_in_ref[k, c, to, :] for k in range(3)], stat_in_ref[3, c, to, :], stat_in_ref[4, c, to, :]

    finish(nrows, ncols, g_ref, acc_ref, stat_in, dyn_ref, chunk_ref, sum_ref, lo, hi)


def fifth_kernel(
    nrows, ncols, lat_ref, w_ref, dyn_in, stat_in_ref, got_ref, sel_ref, col_ref, mean_in,
    stress_ref, damage_ref, mean_ref, g_ref, acc_ref,
):
    load_local(nrows, lat_ref, dyn_in, got_ref, sel_ref, col_ref, mean_in, mean_ref, g_ref)
    nt = g_ref.shape[1]
    smooth_into(w_ref, g_ref, acc_ref, 4, PAD // 8, (PAD + ncols) // 8)
    for c in range(nt):
        w = min(LANES, nrows - c * LANES)
        for i in range(ncols // 8):
            at = slice(PAD + 8 * i, PAD + 8 * i + 8)
            r = stat_in_ref[4, c, PAD - 8 + 8 * i : PAD + 8 * i, :]
            for f in range(4):
                v = (0.5 * g_ref[f, c, at, :] + r * acc_ref[f, c, at, :])[:, 0:w]
                if f == 0:
                    damage_ref[8 * i : 8 * i + 8, c * LANES : c * LANES + w] = v
                else:
                    stress_ref[f - 1, 8 * i : 8 * i + 8, c * LANES : c * LANES + w] = v


def shards(strain_rate, stress_start, concentration, cell_class, land_mask, fold_partner, kernel_weights):
    ncols, nrows = concentration.shape
    nt = -(-nrows // LANES)
    nlon = lax.axis_size("lon")
    nlat = lax.axis_size("lat")
    rows = ncols + 2 * PAD
    mid = rows - 16
    sds = lambda *s: jax.ShapeDtypeStruct(s, F32)
    lat = jnp.stack([lax.axis_index("lat"), jnp.int32(nlat - 1)]).astype(jnp.int32)

    columns = (lax.axis_index("lon") * ncols - PAD + jnp.arange(rows, dtype=jnp.int32)) % (ncols * nlon)
    partner = jnp.take(fold_partner, columns)
    sel = (partner[:, None] // ncols == jnp.arange(nlon)[None, :]).astype(jnp.bfloat16)
    sel = jnp.concatenate([sel, sel, sel], axis=1)
    col = jnp.broadcast_to((partner % ncols)[:, None], (rows, LANES)).astype(jnp.int32)

    f, lat_out, chunk, sums = pl.pallas_call(
        functools.partial(first_kernel, nrows),
        out_shape=(sds(8, nt, ncols, LANES), sds(8, ncols, LANES), sds(5, LANES), sds(8, LANES)),
        in_specs=[SM] + [VM] * 5, out_specs=(VM,) * 4, cost_estimate=cost(4000000, 2000000), name="first",
    )(lat, strain_rate, stress_start, concentration, cell_class, land_mask)
    swap = [(i, nlat - 1 - i) for i in range(nlat)]
    lat_in = lax.ppermute(lat_out, "lat", swap)
    sum_in = lax.ppermute(sums, "lat", swap)
    t8, low, high, send = pl.pallas_call(
        functools.partial(second_kernel, nrows),
        out_shape=(sds(8, ncols, LANES), sds(9, nt, 8, LANES), sds(9, nt, 8, LANES), sds(nlon, 5, LANES)),
        in_specs=[SM] + [VM] * 5, out_specs=(VM,) * 4, cost_estimate=cost(400000, 2000000), name="second",
    )(lat, f, lat_in, chunk, sums, sum_in)
    up = [(i, (i + 1) % nlon) for i in range(nlon)]
    down = [(j, i) for i, j in up]
    high_in = lax.ppermute(high, "lon", up)
    low_in = lax.ppermute(low, "lon", down)
    got = lax.all_to_all(send, "lon", 0, 0, tiled=True).reshape(nlon * 5, LANES)

    scratch = lambda nf: [pltpu.VMEM((nf, nt, rows, LANES), F32), pltpu.VMEM((nf, nt, rows, LANES), F32)]
    dyn, stat, chunk, sums, mean = pl.pallas_call(
        functools.partial(third_kernel, nrows),
        out_shape=(sds(5, nt, mid, LANES), sds(5, nt, mid, LANES), sds(4, LANES), sds(4, LANES), sds(8, LANES)),
        in_specs=[SM, SM] + [VM] * 7, out_specs=(VM,) * 5, scratch_shapes=scratch(5) + [pltpu.VMEM((8, LANES), F32)],
        cost_estimate=cost(40000000, 4000000), name="third",
    )(lat, kernel_weights, f, t8, low_in, high_in, got, sel, col)
    means = [mean[0, 0]]

    def spread(chunk, sums):
        chunk = chunk + lax.ppermute(sums, "lat", swap)
        send = jnp.broadcast_to(chunk[None], (nlon, 4, LANES))
        return lax.all_to_all(send, "lon", 0, 0, tiled=True).reshape(nlon * 4, LANES)

    got = spread(chunk, sums)
    dyn, chunk, sums, mean = pl.pallas_call(
        functools.partial(fourth_kernel, nrows, ncols),
        out_shape=(sds(5, nt, mid, LANES), sds(4, LANES), sds(4, LANES), sds(8, LANES)),
        in_specs=[SM, SM] + [VM] * 6, out_specs=(VM,) * 4, scratch_shapes=scratch(4),
        cost_estimate=cost(30000000, 4000000), name="fourth",
    )(lat, kernel_weights, dyn, stat, got, sel, col, mean)
    means.append(mean[0, 0])
    got = spread(chunk, sums)
    stress, damage, mean = pl.pallas_call(
        functools.partial(fifth_kernel, nrows, ncols),
        out_shape=(sds(3, ncols, nrows), sds(ncols, nrows), sds(8, LANES)),
        in_specs=[SM, SM] + [VM] * 6, out_specs=(VM,) * 3, scratch_shapes=scratch(4),
        cost_estimate=cost(20000000, 4000000), name="fifth",
    )(lat, kernel_weights, dyn, stat, got, sel, col, mean)
    means.append(mean[0, 0])
    return stress, damage, jnp.stack(means)


def solution(mesh):
    in_specs = (
        P(None, "lon", "lat"),
        P(None, "lon", "lat"),
        P("lon", "lat"),
        P(("member", "lon"), "lat"),
        P("lon", "lat"),
        P(),
        P(),
    )
    out_specs = (P(None, ("member", "lon"), "lat"), P(("member", "lon"), "lat"), P("member"))
    return jax.shard_map(shards, mesh=mesh, in_specs=in_specs, out_specs=out_specs, check_vma=False)
```

time: 422 us -> 177 us (0.42)
  other arithmetic: 165 us -> 5.2 us
  starting transfers between devices: 83.8 us -> 40.9 us
  blocking collectives: 72.9 us -> 34.8 us
  Pallas kernels: 0 us -> 32.7 us
  local copies, waits for them, and re-layouts: 27.1 us -> 7.81 us
  waiting for transfers between devices: 65.7 us -> 54.2 us
  between operations: 5.01 us -> 0.73 us
    mul x9 -> x0, other arithmetic: 113 us -> none  [the longest x3 110 us: shards(): fresh = ocean[None] * (0.5 * fields + 0.5 * averaged)]
    all_to_all x2 -> x1, blocking collectives: 72.9 us -> 34.8 us  [spread(): lax.all_to_all(send, 'lon', 0, 0, tiled=True).reshape(nlon * 4, LANES)]
    pallas_call x0 -> x5, Pallas kernels: none -> 32.7 us  [the longest x1 11.7 us: shards(): pl.pallas_call(functools.partial(third_kernel, nrows), out_shape=(sds(5,...]
    div x6 -> x0, other arithmetic: 32.7 us -> none  [the longest x1 32.4 us: shards(): smooth(extend(fields, fold_partner, width), kernel_weights, ncols, nrows)]
    all_to_all x5 -> x2, starting transfers between devices: 61.7 us -> 37.4 us  [the longest x1 32.7 us: shards(): got = lax.all_to_all(send, 'lon', 0, 0, tiled=True).reshape(nlon * 5, LANES)]
    ppermute x16 -> x6, starting transfers between devices: 22.1 us -> 3.45 us  [the longest x1 2.91 us: shards(): low_in = lax.ppermute(low, 'lon', down)]
    all_to_all x5 -> x2, waiting for transfers between devices: 63.2 us -> 51 us  [the longest x1 27.7 us: shards(): got = lax.all_to_all(send, 'lon', 0, 0, tiled=True).reshape(nlon * 5, LANES)]
    gather x5 -> x1, local copies, waits for them, and re-layouts: 9.34 us -> 0.73 us  [shards(): partner = jnp.take(fold_partner, columns)]
  transfers between devices with their start and end apart: 21 -> 8, of which waited for: 5 -> 6; matrix products, arithmetic and copies ran while one was open for 15% -> 3% of each run, Pallas kernels for 0% -> 0%
where the time goes in v1:
time: 177 us; the launch traced here: 176 us
  waiting for transfers between devices  54.2 us (31%)
  starting transfers between devices  40.9 us (23%)
  blocking collectives  34.8 us (20%)
  Pallas kernels  32.7 us (18%)
  local copies, waits for them, and re-layouts  7.81 us (4%)
  other arithmetic  5.2 us (3%)
    all_to_all x1, blocking collectives, spread(): lax.all_to_all(send, 'lon', 0, 0, tiled=True).reshape(nlon * 4, LANES)  34.8 us
    all_to_all x1, starting transfers between devices, shards(): got = lax.all_to_all(send, 'lon', 0, 0, tiled=True).reshape(nlon * 5, LANES)  32.7 us
    all_to_all x1, waiting for transfers between devices, shards(): got = lax.all_to_all(send, 'lon', 0, 0, tiled=True).reshape(nlon * 5, LANES)  27.7 us
    all_to_all x1, waiting for transfers between devices, spread(): lax.all_to_all(send, 'lon', 0, 0, tiled=True).reshape(nlon * 4, LANES)  23.3 us
    pallas_call x1, Pallas kernels, shards(): pl.pallas_call(functools.partial(third_kernel, nrows), out_shape=(sds(5,...  11.7 us
    pallas_call x1, Pallas kernels, shards(): pl.pallas_call(functools.partial(fourth_kernel, nrows, ncols), out_shape=...  10 us
    pallas_call x1, Pallas kernels, shards(): pl.pallas_call(functools.partial(fifth_kernel, nrows, ncols), out_shape=(...  6.17 us
    all_to_all x1, starting transfers between devices, spread(): lax.all_to_all(send, 'lon', 0, 0, tiled=True).reshape(nlon * 4, LANES)  4.77 us
  transfers between devices with their start and end apart: 8, of which 6 were waited for; matrix products, arithmetic and copies ran while one was open for 3% of the time, Pallas kernels for 0%

profile of v1, /device:TPU:38, one launch (start us, length us, event | category | flops | bytes accessed | tf_op | source)
XLA Modules:
  0.0 176.4 jit_solution(10602669264149361258)
XLA Ops:
  0.6 0.0 copy-start
  0.6 0.6 pad_add_fusion.lat_ref
  1.2 2.5 %first.1 = (f32[8,9,32,128]{3,2,1,0:T(8,128)}, f32[8,32,128]{2,1,0:T(8,128)}, f32[5,128]{1,0:T(8,128)}, f32[8,128]{1,0:T(8,128)}) custom-call(s32[2]{0:T(128)} %pad_add_fusion.lat_ref, f32[3,32,1080]{2,1,0:T(8,128)} %strain.1, f32[3,32,1080]{2,1,0:T(8,128)} %stress.1, f32[32,1080]{1,0:T(8,128)} %conc.1, s32[32,1080]{1,0:T(8,128)} %cls.1, s32[32,1080]{1,0:T(8,128)} %mask.1), custom_call_target="tpu_custom_call" | custom-call | flops 4000000 | bytes 2000000 | tf_op jit(solution)/shard_map/first/pallas_call | solution.py:376
  3.7 0.0 collective-permute-start.1
  3.7 0.5 collective-permute-start
  4.3 0.0 copy-done
  4.3 0.7 gather_fusion
  5.0 0.1 collective-permute-done.1.sum_in
  5.1 0.0 copy-start.5
  5.1 0.3 collective-permute-done.lat_in
  5.5 0.0 copy-start.4
  5.5 0.2 copy-done.5
  5.7 0.4 copy-done.4
  6.1 2.4 %second.1 = (f32[8,32,128]{2,1,0:T(8,128)}, f32[9,9,8,128]{3,2,1,0:T(8,128)}, f32[9,9,8,128]{3,2,1,0:T(8,128)}, f32[32,5,128]{2,1,0:T(8,128)}) custom-call(s32[2]{0:T(128)} %pad_add_fusion.lat_ref, f32[8,9,32,128]{3,2,1,0:T(8,128)} %get-tuple-element.23.f_ref, f32[8,32,128]{2,1,0:T(8,128)} %copy-done.4, f32[5,128]{1,0:T(8,128)} %get-tuple-element.25.chunk_ref, ...), custom_call_target="tpu_custom_call" | custom-call | flops 400000 | bytes 2000000 | tf_op jit(solution)/shard_map/second/pallas_call | solution.py:384
  8.5 32.7 %all-to-all-start = ((f32[32,5,128]{2,1,0:T(8,128)}), f32[32,5,128]{2,1,0:T(8,128)S(1)}, u32[]{:S(2)}, u32[]{:S(2)}) async-start(f32[32,5,128]{2,1,0:T(8,128)} %get-tuple-element.30), calls=%async_computation | async-start | bytes 262144 | tf_op jit(solution)/shard_map/all_to_all | solution.py:393
  41.2 2.9 %collective-permute-start.2 = (f32[9,9,8,128]{3,2,1,0:T(8,128)}, f32[9,9,8,128]{3,2,1,0:T(8,128)S(1)}, u32[]{:S(2)}, u32[]{:S(2)}) collective-permute-start(f32[9,9,8,128]{3,2,1,0:T(8,128)} %get-tuple-element.28), channel_id=1, source_target_pairs={{2,0},{4,2},{6,4},{8,6},{10,8},{12,10},{14,12},{16,14},{18,16},{20... | collective-permute-start | bytes 995336 | tf_op jit(solution)/shard_map/ppermute | solution.py:392
  44.1 0.0 collective-permute-start.3
  44.1 0.1 iota_compare_fusion
  44.2 0.7 add_convert_fusion.sel_ref
  44.9 27.7 %all-to-all-done = f32[32,5,128]{2,1,0:T(8,128)S(1)} async-done(((f32[32,5,128]{2,1,0:T(8,128)}), f32[32,5,128]{2,1,0:T(8,128)S(1)}, u32[]{:S(2)}, u32[]{:S(2)}) %all-to-all-start) | async-done | bytes 81952 | tf_op jit(solution)/shard_map/all_to_all | solution.py:393
  72.6 0.6 reshape.127.got_ref
  73.2 0.0 collective-permute-done.2.low_in
  73.2 0.0 copy-start.1
  73.2 0.0 collective-permute-done.3.high_in
  73.2 0.0 copy-start.2
  73.2 0.8 broadcast_in_dim.13.col_ref
  74.0 0.0 copy-done.1
  74.0 0.0 copy-done.2
  74.1 11.7 %third.1 = (f32[5,9,48,128]{3,2,1,0:T(8,128)}, f32[5,9,48,128]{3,2,1,0:T(8,128)}, f32[4,128]{1,0:T(4,128)}, f32[4,128]{1,0:T(4,128)}, f32[8,128]{1,0:T(8,128)}) custom-call(s32[2]{0:T(128)} %pad_add_fusion.lat_ref, f32[7,7]{1,0:T(8,128)} %w_ref.5, f32[8,9,32,128]{3,2,1,0:T(8,128)} %get-tuple-element.23.f_ref, f32[8,32,128]{2,1,0:T(8,128)} %get-tuple-element.27.t8_ref, ...), custom_call_target="tpu_custom_call" | custom-call | flops 40000000 | bytes 4000000 | tf_op jit(solution)/shard_map/third/pallas_call | solution.py:396
  85.7 0.0 collective-permute-start.4
  85.8 1.4 collective-permute-done.4
  87.1 0.7 add.101
  87.8 34.8 %all_to_all.15 = f32[32,4,128]{2,1,0:T(4,128)} all-to-all(f32[32,4,128]{2,1,0:T(4,128)S(1)} %broadcast_in_dim.14), channel_id=1, replica_groups=mesh['member'=4,'lon'=32,'lat'=2] {'lon'}, dimensions={0} | all-to-all | bytes 131072 | tf_op jit(solution)/shard_map/all_to_all | solution.py:407
  122.6 10.0 %fourth.1 = (f32[5,9,48,128]{3,2,1,0:T(8,128)}, f32[4,128]{1,0:T(4,128)}, f32[4,128]{1,0:T(4,128)}, f32[8,128]{1,0:T(8,128)}) custom-call(s32[2]{0:T(128)} %pad_add_fusion.lat_ref, f32[7,7]{1,0:T(8,128)} %w_ref.5, f32[5,9,48,128]{3,2,1,0:T(8,128)} %get-tuple-element.31.dyn_in, f32[5,9,48,128]{3,2,1,0:T(8,128)} %get-tuple-element.32.stat_in_ref, ...), custom_call_target="tpu_custom_call" | custom-call | flops 30000000 | bytes 4000000 | tf_op jit(solution)/shard_map/fourth/pallas_call | solution.py:410
  132.7 0.0 collective-permute-start.5
  132.7 1.4 collective-permute-done.5
  134.0 0.7 add.102
  134.7 0.6 broadcast_in_dim.15
  135.4 4.8 %all-to-all-start.2 = ((f32[32,4,128]{2,1,0:T(4,128)}), f32[32,4,128]{2,1,0:T(4,128)S(1)}, u32[]{:S(2)}, u32[]{:S(2)}) async-start(f32[32,4,128]{2,1,0:T(4,128)} %broadcast_in_dim.15), calls=%async_computation.2 | async-start | bytes 131072 | tf_op jit(solution)/shard_map/all_to_all | solution.py:407
  140.1 1.2 slice.9
  141.3 1.2 slice.10
  142.5 23.3 %all-to-all-done.2 = f32[32,4,128]{2,1,0:T(4,128)S(1)} async-done(((f32[32,4,128]{2,1,0:T(4,128)}), f32[32,4,128]{2,1,0:T(4,128)S(1)}, u32[]{:S(2)}, u32[]{:S(2)}) %all-to-all-start.2) | async-done | bytes 65568 | tf_op jit(solution)/shard_map/all_to_all | solution.py:407
  165.9 0.0 copy-start.3
  165.9 0.6 copy-done.3
  166.5 6.2 %fifth.1 = (f32[3,32,1080]{2,1,0:T(8,128)}, f32[32,1080]{1,0:T(8,128)}, f32[8,128]{1,0:T(8,128)}) custom-call(s32[2]{0:T(128)} %pad_add_fusion.lat_ref, f32[7,7]{1,0:T(8,128)} %w_ref.5, f32[5,9,48,128]{3,2,1,0:T(8,128)} %get-tuple-element.36.dyn_in, f32[5,9,48,128]{3,2,1,0:T(8,128)} %get-tuple-element.32.stat_in_ref, f32[128,128]{1,0:T(8,128)} %bitcast.8, ...), custom_call_target="tpu_custom_call" | custom-call | flops 20000000 | bytes 4000000 | tf_op jit(solution)/shard_map/fifth/pallas_call | solution.py:418
  172.7 1.2 slice.11
  173.9 2.4 %pad_maximum_fusion = f32[3]{0:T(128)} fusion(f32[1]{0:T(128)} %bitcast.6, f32[1]{0:T(128)} %bitcast.5, f32[1]{0:T(128)} %bitcast.4), kind=kLoop, calls=%fused_computation.22 | loop fusion | flops 6 | bytes 24 | tf_op jit(solution)/shard_map/stack | solution.py:425
  (5 shorter events, 0.1 us)
Async XLA Ops:
  0.6 3.7 %copy-start = (s32[1024]{0:T(1024)S(1)}, s32[1024]{0:T(1024)}, u32[]{:S(2)}) copy-start(s32[1024]{0:T(1024)} %param.12) | copy-start | bytes 12292
  3.7 1.4 collective-permute-start.1
  3.7 1.7 collective-permute-start
  5.1 0.6 copy-start.5
  5.5 0.7 copy-start.4
  8.5 64.1 %all-to-all-start = ((f32[32,5,128]{2,1,0:T(8,128)}), f32[32,5,128]{2,1,0:T(8,128)S(1)}, u32[]{:S(2)}, u32[]{:S(2)}) async-start(f32[32,5,128]{2,1,0:T(8,128)} %get-tuple-element.30), calls=%async_computation | async-start | bytes 262144 | tf_op jit(solution)/shard_map/all_to_all | solution.py:393
  41.2 32.0 %collective-permute-start.2 = (f32[9,9,8,128]{3,2,1,0:T(8,128)}, f32[9,9,8,128]{3,2,1,0:T(8,128)S(1)}, u32[]{:S(2)}, u32[]{:S(2)}) collective-permute-start(f32[9,9,8,128]{3,2,1,0:T(8,128)} %get-tuple-element.28), channel_id=1, source_target_pairs={{2,0},{4,2},{6,4},{8,6},{10,8},{12,10},{14,12},{16,14},{18,16},{20... | collective-permute-start | bytes 995336 | tf_op jit(solution)/shard_map/ppermute | solution.py:392
  44.1 29.1 %collective-permute-start.3 = (f32[9,9,8,128]{3,2,1,0:T(8,128)}, f32[9,9,8,128]{3,2,1,0:T(8,128)S(1)}, u32[]{:S(2)}, u32[]{:S(2)}) collective-permute-start(f32[9,9,8,128]{3,2,1,0:T(8,128)} %get-tuple-element.29), channel_id=1, source_target_pairs={{0,2},{2,4},{4,6},{6,8},{8,10},{10,12},{12,14},{14,16},{16,18},{18... | collective-permute-start | bytes 995336 | tf_op jit(solution)/shard_map/ppermute | solution.py:391
  73.2 0.8 copy-start.1
  73.2 0.9 copy-start.2
  85.7 1.4 collective-permute-start.4
  132.7 1.4 collective-permute-start.5
  135.4 30.5 %all-to-all-start.2 = ((f32[32,4,128]{2,1,0:T(4,128)}), f32[32,4,128]{2,1,0:T(4,128)S(1)}, u32[]{:S(2)}, u32[]{:S(2)}) async-start(f32[32,4,128]{2,1,0:T(4,128)} %broadcast_in_dim.15), calls=%async_computation.2 | async-start | bytes 131072 | tf_op jit(solution)/shard_map/all_to_all | solution.py:407
  165.9 0.6 copy-start.3

commit v2 on v1

--- a/solution.py
+++ b/solution.py
@@ -6,6 +6,7 @@
 from jax.experimental.pallas import tpu as pltpu
 from jax.sharding import PartitionSpec as P
 
+
 ITERS = 3
 HALO = 9
 LANES = 128
@@ -15,8 +16,23 @@
 SM = pl.BlockSpec(memory_space=pltpu.SMEM)
 
 
+def small():
+    return pltpu.CompilerParams(vmem_limit_bytes=12 * 1024 * 1024)
+
+
+def is_north():
+    return lax.axis_index("lat") == lax.axis_size("lat") - 1
+
+
 def cost(flops, size):
     return pl.CostEstimate(flops=flops, bytes_accessed=size, transcendentals=0)
+
+
+def overstress(e, rc):
+    half = (e[0] - e[1]) * 0.5
+    tau = jnp.sqrt(half * half + e[2] * e[2] + 0.25)
+    over = jnp.maximum((tau + 0.35 * (e[0] + e[1])) * rc, 1.0)
+    return over - 1.0, 1.0 - 1.0 / over
 
 
 def physics(damage, stress, bl, rc, oc):
@@ -24,33 +40,33 @@
     k2 = keep * keep
     g = oc * (k2 / (k2 + 0.5))
     e = [g * (stress[k] + keep * bl[k]) for k in range(3)]
-    half = (e[0] - e[1]) * 0.5
-    tau = jnp.sqrt(half * half + e[2] * e[2] + 0.25)
-    over = jnp.maximum((tau + 0.35 * (e[0] + e[1])) * rc, 1.0)
-    q = oc * (1.0 - 1.0 / over)
-    return e, q, oc * (over - 1.0)
-
-
-def tops(tiles, single, extra, at):
+    excess, q = overstress(e, rc)
+    return e, oc * q, oc * excess
+
+
+def tops(tiles, single, at):
     t = jnp.concatenate(tiles, axis=0).T
     rows = [t[at - k : at - k + 1, :] for k in range(3)]
-    for one in (single, extra):
-        if one is not None:
-            parts = [one] + [pltpu.roll(one, k, 1) for k in (1, 2)] + [jnp.zeros_like(one)]
-            rows.append(jnp.concatenate(parts, axis=0).T[at : at + 1, :])
-    return rows
+    parts = [single] + [pltpu.roll(single, k, 1) for k in (1, 2)] + [jnp.zeros_like(single)]
+    return rows + [jnp.concatenate(parts, axis=0).T[at : at + 1, :]]
 
 
 def total(x):
     return jnp.sum(jnp.sum(x, axis=0, keepdims=True), axis=1, keepdims=True)
 
 
-def first_kernel(nrows, lat_ref, strain, stress, conc, cls, mask, f_ref, lat_out, chunk_ref, sum_ref):
+def first_kernel(nrows, *refs):
+    given, (f_ref, lat_out, chunk_ref, sum_ref), held, sem = refs[:5], refs[5:9], refs[9:14], refs[14]
+    copies = [pltpu.make_async_copy(a, b, sem.at[n]) for n, (a, b) in enumerate(zip(given, held, strict=True))]
+    for copy in copies:
+        copy.start()
+    for copy in copies:
+        copy.wait()
+    strain, stress, conc, cls, mask = held
     nt = f_ref.shape[1]
     ncols = conc.shape[0]
     excess = jnp.zeros((ncols, LANES), F32)
     count = jnp.zeros((ncols, LANES), F32)
-    last = {}
     lane = lax.broadcasted_iota(jnp.int32, (ncols, LANES), 1)
     f_ref[:, nt - 1] = jnp.zeros((8, ncols, LANES), F32)
     for c in range(nt):
@@ -76,11 +92,11 @@
         d = f_ref[7, c]
         oc = jnp.where(mc > 0.0, 1.0, 0.0)
         rc = 1.0 / (0.6 * jnp.where(mc > 0.0, mc, 1.0))
-        e, q, over = physics(d, st, bl, rc, oc)
+        e, _, over = physics(d, st, bl, rc, oc)
         excess = excess + over
         count = count + oc
     at = nrows - 1 - (nt - 1) * LANES
-    rows = tops([d, q, e[0], e[1]], e[2], oc, at)
+    rows = tops([d, mc, e[0], e[1]], e[2], at)
     s = total(excess)
     n = total(count)
     lane1 = lax.broadcasted_iota(jnp.int32, (1, LANES), 1)
@@ -88,17 +104,17 @@
     for k, row in enumerate(rows):
         chunk_ref[k : k + 1, :] = row
     sum_ref[...] = jnp.broadcast_to(sums, sum_ref.shape)
-    north = lat_ref[0] == lat_ref[1]
+    north = is_north()
     for f in range(8):
         lat_out[f] = jnp.where(north, f_ref[f, 0], f_ref[f, nt - 1])
 
 
-def second_kernel(nrows, lat_ref, f_ref, lat_in, chunk_ref, sum_ref, sum_in, t8_ref, low_ref, high_ref, send_ref):
+def second_kernel(nrows, f_ref, lat_in, chunk_ref, sum_ref, sum_in, t8_ref, low_ref, high_ref, send_ref):
     nt = f_ref.shape[1]
     ncols = f_ref.shape[2]
     edge = nrows - (nt - 1) * LANES
     lane = lax.broadcasted_iota(jnp.int32, (ncols, LANES), 1)
-    north = lat_ref[0] == lat_ref[1]
+    north = is_north()
     own = lane < edge
     keep = jnp.where(north, (lane >= LANES - HALO).astype(jnp.int32), ((lane >= edge) & (lane < edge + HALO)).astype(jnp.int32)) > 0
     for f in range(8):
@@ -112,18 +128,18 @@
             high_ref[f, c] = at[ncols - 8 : ncols]
             high_ref[8, c, f : f + 1] = at[ncols - 9 : ncols - 8]
     s = sum_ref[0:1, :] + sum_in[0:1, :]
-    chunk = [chunk_ref[k : k + 1, :] for k in range(5)]
+    chunk = [chunk_ref[k : k + 1, :] for k in range(4)]
     chunk[3] = chunk[3] + s
     block = jnp.concatenate(chunk, axis=0)
     for n in range(send_ref.shape[0]):
         send_ref[n] = block
 
 
-def ghosts(got_ref, sel_ref, col_ref, per, fields):
-    n = got_ref.shape[0] // per
+def ghosts(got_ref, sel_ref, col_ref):
+    n = got_ref.shape[0] // 4
     parts = []
-    for r in range(per):
-        m = got_ref[pl.ds(r, n, stride=per), :]
+    for r in range(4):
+        m = got_ref[pl.ds(r, n, stride=4), :]
         h = m.astype(jnp.bfloat16)
         m = m - h.astype(F32)
         h2 = m.astype(jnp.bfloat16)
@@ -133,12 +149,12 @@
     lane = lax.broadcasted_iota(jnp.int32, (sel_ref.shape[0], LANES), 1)
     col = col_ref[...] == (lane & 31)
     group = lane >> 5
-    picked = [jnp.where(col, picked[:, r * LANES : (r + 1) * LANES], 0.0) for r in range(per)]
+    picked = [jnp.where(col, picked[:, r * LANES : (r + 1) * LANES], 0.0) for r in range(4)]
     out = []
-    for f in range(fields):
+    for f in range(5):
         vals = []
         for k in range(3):
-            row, g = (k, f) if f < 4 else (3 + f - 4, k)
+            row, g = (k, f) if f < 4 else (3, k)
             vals.append(jnp.sum(jnp.where(group == g, picked[row], 0.0), axis=1, keepdims=True))
         out.append(vals)
     return out
@@ -151,7 +167,7 @@
     def body(step, _):
         f = step // (hi - lo)
         row = (lo + step % (hi - lo)) * 8
-        mid, rolled, out = {}, {}, {}
+        mid, rolled = {}, {}
         for c in range(nt):
             x = [g_ref[f, c, pl.ds(row + a - 3, 8), :] for a in range(7)]
             for b in range(7):
@@ -174,18 +190,22 @@
     lax.fori_loop(0, nf * (hi - lo), body, 0)
 
 
-def put_ghosts(lat_ref, g_ref, gh, factor, nrows, row0, nrow, with_ocean):
+def put_ghosts(g_ref, gh, factor, nrows, row0, nrow, first):
     nt = g_ref.shape[1]
     edge = nrows - (nt - 1) * LANES
     lane = lax.broadcasted_iota(jnp.int32, (nrow, LANES), 1)
-    north = (lat_ref[0] == lat_ref[1]).astype(jnp.int32)
+    north = is_north().astype(jnp.int32)
     vals = []
     d, q = gh[0], gh[1]
+    if first:
+        oc = [jnp.where(v > 0.0, 1.0, 0.0) for v in q]
+        rc = [1.0 / (0.6 * jnp.where(v > 0.0, v, 1.0)) for v in q]
+        q = [oc[k] * overstress([gh[2 + m][k] for m in range(3)], rc[k])[1] for k in range(3)]
     vals.append([d[k] + factor * (1.0 - d[k]) * q[k] for k in range(3)])
     for m in range(3):
         vals.append([gh[2 + m][k] * (1.0 - factor * q[k]) for k in range(3)])
-    if with_ocean:
-        vals.append(gh[5])
+    if first:
+        vals.append(oc)
     for f, v in enumerate(vals):
         t = g_ref[f, nt - 1, row0 : row0 + nrow, :]
         for k in range(3):
@@ -236,24 +256,24 @@
         excess = lax.fori_loop(lo, hi, body, excess)
     own = slice(PAD - lo * 8, PAD - lo * 8 + ncols)
     tile = [dyn_ref[f, nt - 1, own, :] for f in range(5)]
-    rows = tops(tile[:4], tile[4], None, edge - 1)
+    rows = tops(tile[:4], tile[4], edge - 1)
     step_sums(chunk_ref, sum_ref, rows, excess)
 
 
 def third_kernel(
-    nrows, lat_ref, w_ref, f_ref, t8_ref, low_in, high_in, got_ref, sel_ref, col_ref,
+    nrows, w_ref, f_ref, t8_ref, low_in, high_in, got_ref, sel_ref, col_ref,
     dyn_ref, stat_ref, chunk_ref, sum_ref, mean_ref, g_ref, acc_ref, rc_ref,
 ):
     nt = f_ref.shape[1]
     ncols = f_ref.shape[2]
     rows = g_ref.shape[2]
-    n = got_ref.shape[0] // 5
-    sums = jnp.sum(got_ref[pl.ds(3, n, stride=5), :], axis=0, keepdims=True)
+    n = got_ref.shape[0] // 4
+    sums = jnp.sum(got_ref[pl.ds(3, n, stride=4), :], axis=0, keepdims=True)
     count = lane_value(sums, 97) + 1.0
     mean = lane_value(sums, 96) / count
     factor = 1.0 / (1.0 + 2.0 * mean)
     lane1 = lax.broadcasted_iota(jnp.int32, (1, LANES), 1)
-    mean_ref[...] = jnp.broadcast_to(jnp.where(lane1 == 0, mean, count), mean_ref.shape)
+    mean_ref[...] = jnp.broadcast_to(jnp.where(lane1 == 1, mean, count), mean_ref.shape)
     factor8 = jnp.broadcast_to(factor, (8, LANES))
     lo, hi = 1, rows // 8 - 1
     for c in range(nt):
@@ -281,10 +301,10 @@
             local([(t8_ref[f, 8 * i : 8 * i + 8, :] if c == nt - 1 else f_ref[f, c, 8 * i : 8 * i + 8, :]) for f in range(8)], PAD + 8 * i, 8)
         local([low_in[f, c] for f in range(8)], PAD + ncols, 8)
         local([low_in[8, c, f : f + 1, :] for f in range(8)], PAD + ncols + 8, 1)
-    gh = ghosts(got_ref, sel_ref, col_ref, 5, 6)
+    gh = ghosts(got_ref, sel_ref, col_ref)
     for i in range(lo, hi):
         stat_ref[4, nt - 1, 8 * (i - lo) : 8 * (i - lo) + 8, :] = g_ref[4, nt - 1, 8 * i : 8 * i + 8, :]
-    put_ghosts(lat_ref, g_ref, gh, factor, nrows, 0, rows, True)
+    put_ghosts(g_ref, gh, factor, nrows, 0, rows, True)
     smooth_into(w_ref, g_ref, acc_ref, 5, lo, hi)
 
     def stat_in(c, at, to):
@@ -296,15 +316,12 @@
     finish(nrows, ncols, g_ref, acc_ref, stat_in, dyn_ref, chunk_ref, sum_ref, lo, hi)
 
 
-def load_local(nrows, lat_ref, dyn_in, got_ref, sel_ref, col_ref, mean_in, mean_ref, g_ref):
+def load_local(nrows, dyn_in, got_ref, sel_ref, col_ref, mean_in, g_ref):
     nt = g_ref.shape[1]
     n = got_ref.shape[0] // 4
     sums = jnp.sum(got_ref[pl.ds(3, n, stride=4), :], axis=0, keepdims=True)
-    count = lane_value(mean_in[0:1, :], 1)
-    mean = lane_value(sums, 96) / count
+    mean = lane_value(sums, 96) / lane_value(mean_in[0:1, :], 0)
     factor = 1.0 / (1.0 + 2.0 * mean)
-    lane1 = lax.broadcasted_iota(jnp.int32, (1, LANES), 1)
-    mean_ref[...] = jnp.broadcast_to(jnp.where(lane1 == 0, mean, count), mean_ref.shape)
     f8 = jnp.broadcast_to(factor, (8, LANES))
     for c in range(nt):
 
@@ -319,15 +336,18 @@
             return 0
 
         lax.fori_loop(0, dyn_in.shape[2] // 8, body, 0)
-    gh = ghosts(got_ref, sel_ref, col_ref, 4, 5)
-    put_ghosts(lat_ref, g_ref, gh, factor, nrows, 0, g_ref.shape[2], False)
+    gh = ghosts(got_ref, sel_ref, col_ref)
+    put_ghosts(g_ref, gh, factor, nrows, 0, g_ref.shape[2], False)
+    return mean
 
 
 def fourth_kernel(
-    nrows, ncols, lat_ref, w_ref, dyn_in, stat_in_ref, got_ref, sel_ref, col_ref, mean_in,
+    nrows, ncols, w_ref, dyn_in, stat_in_ref, got_ref, sel_ref, col_ref, mean_in,
     dyn_ref, chunk_ref, sum_ref, mean_ref, g_ref, acc_ref,
 ):
-    load_local(nrows, lat_ref, dyn_in, got_ref, sel_ref, col_ref, mean_in, mean_ref, g_ref)
+    mean = load_local(nrows, dyn_in, got_ref, sel_ref, col_ref, mean_in, g_ref)
+    lane = lax.broadcasted_iota(jnp.int32, mean_ref.shape, 1)
+    mean_ref[...] = jnp.where(lane == 2, mean, mean_in[...])
     lo, hi = 1, g_ref.shape[2] // 8 - 1
     smooth_into(w_ref, g_ref, acc_ref, 4, lo, hi)
 
@@ -338,10 +358,13 @@
 
 
 def fifth_kernel(
-    nrows, ncols, lat_ref, w_ref, dyn_in, stat_in_ref, got_ref, sel_ref, col_ref, mean_in,
+    nrows, ncols, w_ref, dyn_in, stat_in_ref, got_ref, sel_ref, col_ref, mean_in,
     stress_ref, damage_ref, mean_ref, g_ref, acc_ref,
 ):
-    load_local(nrows, lat_ref, dyn_in, got_ref, sel_ref, col_ref, mean_in, mean_ref, g_ref)
+    mean = load_local(nrows, dyn_in, got_ref, sel_ref, col_ref, mean_in, g_ref)
+    row = mean_in[0:1, :]
+    for at, one in enumerate((lane_value(row, 1), lane_value(row, 2), mean)):
+        mean_ref[at] = jnp.sum(one)
     nt = g_ref.shape[1]
     smooth_into(w_ref, g_ref, acc_ref, 4, PAD // 8, (PAD + ncols) // 8)
     for c in range(nt):
@@ -365,7 +388,6 @@
     rows = ncols + 2 * PAD
     mid = rows - 16
     sds = lambda *s: jax.ShapeDtypeStruct(s, F32)
-    lat = jnp.stack([lax.axis_index("lat"), jnp.int32(nlat - 1)]).astype(jnp.int32)
 
     columns = (lax.axis_index("lon") * ncols - PAD + jnp.arange(rows, dtype=jnp.int32)) % (ncols * nlon)
     partner = jnp.take(fold_partner, columns)
@@ -373,33 +395,35 @@
     sel = jnp.concatenate([sel, sel, sel], axis=1)
     col = jnp.broadcast_to((partner % ncols)[:, None], (rows, LANES)).astype(jnp.int32)
 
+    given = (strain_rate, stress_start, concentration, cell_class, land_mask)
     f, lat_out, chunk, sums = pl.pallas_call(
         functools.partial(first_kernel, nrows),
-        out_shape=(sds(8, nt, ncols, LANES), sds(8, ncols, LANES), sds(5, LANES), sds(8, LANES)),
-        in_specs=[SM] + [VM] * 5, out_specs=(VM,) * 4, cost_estimate=cost(4000000, 2000000), name="first",
-    )(lat, strain_rate, stress_start, concentration, cell_class, land_mask)
+        out_shape=(sds(8, nt, ncols, LANES), sds(8, ncols, LANES), sds(4, LANES), sds(8, LANES)),
+        in_specs=[pl.BlockSpec(memory_space=pltpu.HBM)] * 5, out_specs=(VM,) * 4,
+        scratch_shapes=[pltpu.VMEM(a.shape, a.dtype) for a in given] + [pltpu.SemaphoreType.DMA((5,))],
+        cost_estimate=cost(4000000, 2000000), compiler_params=small(), name="first",
+    )(*given)
     swap = [(i, nlat - 1 - i) for i in range(nlat)]
     lat_in = lax.ppermute(lat_out, "lat", swap)
     sum_in = lax.ppermute(sums, "lat", swap)
     t8, low, high, send = pl.pallas_call(
         functools.partial(second_kernel, nrows),
-        out_shape=(sds(8, ncols, LANES), sds(9, nt, 8, LANES), sds(9, nt, 8, LANES), sds(nlon, 5, LANES)),
-        in_specs=[SM] + [VM] * 5, out_specs=(VM,) * 4, cost_estimate=cost(400000, 2000000), name="second",
-    )(lat, f, lat_in, chunk, sums, sum_in)
+        out_shape=(sds(8, ncols, LANES), sds(9, nt, 8, LANES), sds(9, nt, 8, LANES), sds(nlon, 4, LANES)),
+        in_specs=[VM] * 5, out_specs=(VM,) * 4, cost_estimate=cost(400000, 2000000), compiler_params=small(), name="second",
+    )(f, lat_in, chunk, sums, sum_in)
     up = [(i, (i + 1) % nlon) for i in range(nlon)]
     down = [(j, i) for i, j in up]
     high_in = lax.ppermute(high, "lon", up)
     low_in = lax.ppermute(low, "lon", down)
-    got = lax.all_to_all(send, "lon", 0, 0, tiled=True).reshape(nlon * 5, LANES)
+    got = lax.all_to_all(send, "lon", 0, 0, tiled=True).reshape(nlon * 4, LANES)
 
     scratch = lambda nf: [pltpu.VMEM((nf, nt, rows, LANES), F32), pltpu.VMEM((nf, nt, rows, LANES), F32)]
     dyn, stat, chunk, sums, mean = pl.pallas_call(
         functools.partial(third_kernel, nrows),
         out_shape=(sds(5, nt, mid, LANES), sds(5, nt, mid, LANES), sds(4, LANES), sds(4, LANES), sds(8, LANES)),
-        in_specs=[SM, SM] + [VM] * 7, out_specs=(VM,) * 5, scratch_shapes=scratch(5) + [pltpu.VMEM((8, LANES), F32)],
-        cost_estimate=cost(40000000, 4000000), name="third",
-    )(lat, kernel_weights, f, t8, low_in, high_in, got, sel, col)
-    means = [mean[0, 0]]
+        in_specs=[SM] + [VM] * 7, out_specs=(VM,) * 5, scratch_shapes=scratch(5) + [pltpu.VMEM((8, LANES), F32)],
+        cost_estimate=cost(40000000, 4000000), compiler_params=small(), name="third",
+    )(kernel_weights, f, t8, low_in, high_in, got, sel, col)
 
     def spread(chunk, sums):
         chunk = chunk + lax.ppermute(sums, "lat", swap)
@@ -410,19 +434,17 @@
     dyn, chunk, sums, mean = pl.pallas_call(
         functools.partial(fourth_kernel, nrows, ncols),
         out_shape=(sds(5, nt, mid, LANES), sds(4, LANES), sds(4, LANES), sds(8, LANES)),
-        in_specs=[SM, SM] + [VM] * 6, out_specs=(VM,) * 4, scratch_shapes=scratch(4),
-        cost_estimate=cost(30000000, 4000000), name="fourth",
-    )(lat, kernel_weights, dyn, stat, got, sel, col, mean)
-    means.append(mean[0, 0])
+        in_specs=[SM] + [VM] * 6, out_specs=(VM,) * 4, scratch_shapes=scratch(4),
+        cost_estimate=cost(30000000, 4000000), compiler_params=small(), name="fourth",
+    )(kernel_weights, dyn, stat, got, sel, col, mean)
     got = spread(chunk, sums)
     stress, damage, mean = pl.pallas_call(
         functools.partial(fifth_kernel, nrows, ncols),
-        out_shape=(sds(3, ncols, nrows), sds(ncols, nrows), sds(8, LANES)),
-        in_specs=[SM, SM] + [VM] * 6, out_specs=(VM,) * 3, scratch_shapes=scratch(4),
-        cost_estimate=cost(20000000, 4000000), name="fifth",
-    )(lat, kernel_weights, dyn, stat, got, sel, col, mean)
-    means.append(mean[0, 0])
-    return stress, damage, jnp.stack(means)
+        out_shape=(sds(3, ncols, nrows), sds(ncols, nrows), sds(ITERS)),
+        in_specs=[SM] + [VM] * 6, out_specs=(VM, VM, SM), scratch_shapes=scratch(4),
+        cost_estimate=cost(20000000, 4000000), compiler_params=small(), name="fifth",
+    )(kernel_weights, dyn, stat, got, sel, col, mean)
+    return stress, damage, mean
 
 
 def solution(mesh):

time: 177 us -> 159 us (0.90)
  blocking collectives: 34.8 us -> 64.9 us
  waiting for transfers between devices: 54.2 us -> 25.3 us
  Pallas kernels: 32.7 us -> 25.2 us
  other arithmetic: 5.2 us -> 0.22 us
  starting transfers between devices: 40.9 us -> 36.5 us
  local copies, waits for them, and re-layouts: 7.81 us -> 5.6 us
    all_to_all x2 -> x1, waiting for transfers between devices: 51 us -> 9.1 us  [shards(): got = lax.all_to_all(send, 'lon', 0, 0, tiled=True).reshape(nlon * 4, LANES)]
    all_to_all x1 -> x2, blocking collectives: 34.8 us -> 64.9 us  [spread(): lax.all_to_all(send, 'lon', 0, 0, tiled=True).reshape(nlon * 4, LANES)]
    ppermute x1, waiting for transfers between devices: 0.01 us -> 11.4 us  [shards(): low_in = lax.ppermute(low, 'lon', down)]
    all_to_all x2 -> x1, starting transfers between devices: 37.4 us -> 32.7 us  [shards(): got = lax.all_to_all(send, 'lon', 0, 0, tiled=True).reshape(nlon * 4, LANES)]
    slice x3 -> x0, local copies, waits for them, and re-layouts: 3.65 us -> none  [the longest x2 2.46 us: shards(): means.append(mean[0, 0])]
    unnamed x12 -> x14, local copies, waits for them, and re-layouts: 1.31 us -> 4.77 us
    another operation x2 -> x0, other arithmetic: 3.02 us -> none  [the longest x1 2.42 us: shards(): return (stress, damage, jnp.stack(means))]
    ppermute x1, waiting for transfers between devices: 0.01 us -> 2.33 us  [shards(): high_in = lax.ppermute(high, 'lon', up)]
  transfers between devices with their start and end apart: 8 -> 7, of which waited for: 6 -> 6; matrix products, arithmetic and copies ran while one was open for 3% -> 1% of each run, Pallas kernels for 0% -> 0%
where the time goes in v2:
time: 159 us; the launch traced here: 158 us
  blocking collectives  64.9 us (41%)
  starting transfers between devices  36.5 us (23%)
  waiting for transfers between devices  25.3 us (16%)
  Pallas kernels  25.2 us (16%)
  local copies, waits for them, and re-layouts  5.6 us (4%)
    all_to_all x2, blocking collectives, spread(): lax.all_to_all(send, 'lon', 0, 0, tiled=True).reshape(nlon * 4, LANES)  64.9 us
    all_to_all x1, starting transfers between devices, shards(): got = lax.all_to_all(send, 'lon', 0, 0, tiled=True).reshape(nlon * 4, LANES)  32.7 us
    ppermute x1, waiting for transfers between devices, shards(): low_in = lax.ppermute(low, 'lon', down)  11.4 us
    pallas_call x1, Pallas kernels, shards(): pl.pallas_call(functools.partial(third_kernel, nrows), out_shape=(sds(5,...  9.63 us
    all_to_all x1, waiting for transfers between devices, shards(): got = lax.all_to_all(send, 'lon', 0, 0, tiled=True).reshape(nlon * 4, LANES)  9.1 us
    pallas_call x1, Pallas kernels, shards(): pl.pallas_call(functools.partial(fourth_kernel, nrows, ncols), out_shape=...  8.07 us
    pallas_call x1, Pallas kernels, shards(): pl.pallas_call(functools.partial(fifth_kernel, nrows, ncols), out_shape=(...  5.22 us
    unnamed x14, local copies, waits for them, and re-layouts  4.77 us
  transfers between devices with their start and end apart: 7, of which 6 were waited for; matrix products, arithmetic and copies ran while one was open for 1% of the time, Pallas kernels for 0%

profile of v2, /device:TPU:38, one launch (start us, length us, event | category | flops | bytes accessed | tf_op | source)
XLA Modules:
  0.0 158.4 jit_solution(9579173486229586330)
XLA Ops:
  0.6 0.0 copy-start
  0.6 0.0 copy-start.1
  0.7 1.0 copy-done.1
  1.7 0.0 copy-start.2
  1.7 1.0 copy-done.2
  2.7 0.0 copy-start.3
  2.7 0.9 copy-done.3
  3.6 0.0 copy-start.4
  3.6 0.9 copy-done.4
  4.5 0.0 copy-start.5
  4.5 0.9 copy-done.5
  5.4 1.6 %first.1 = (f32[8,9,32,128]{3,2,1,0:T(8,128)S(1)}, f32[8,32,128]{2,1,0:T(8,128)S(1)}, f32[4,128]{1,0:T(4,128)S(1)}, f32[8,128]{1,0:T(8,128)S(1)}) custom-call(f32[3,32,1080]{2,1,0:T(8,128)S(1)} %copy-done.1, f32[3,32,1080]{2,1,0:T(8,128)S(1)} %copy-done.2, f32[32,1080]{1,0:T(8,128)S(1)} %copy-done.3, s32[32,1080]{1,0:T(8,128)S(1)} %copy-done.4, ...), custom_call_target="tpu_custom_call" | custom-call | flops 4000000 | bytes 2000000 | tf_op jit(solution)/shard_map/first/pallas_call | solution.py:399
  7.0 0.0 copy-start.6
  7.1 0.1 collective-permute-start.1
  7.2 0.5 collective-permute-start
  7.7 0.0 copy-done
  7.7 0.7 gather_fusion
  8.5 0.0 collective-permute-done.1.sum_in
  8.5 0.2 collective-permute-done.lat_in
  8.7 0.7 second.1
  9.4 32.7 %all-to-all-start = ((f32[32,4,128]{2,1,0:T(4,128)}), f32[32,4,128]{2,1,0:T(4,128)S(1)}, u32[]{:S(2)}, u32[]{:S(2)}) async-start(f32[32,4,128]{2,1,0:T(4,128)} %get-tuple-element.27), calls=%async_computation | async-start | bytes 131072 | tf_op jit(solution)/shard_map/all_to_all | solution.py:418
  42.0 2.9 %collective-permute-start.2 = (f32[9,9,8,128]{3,2,1,0:T(8,128)S(1)}, f32[9,9,8,128]{3,2,1,0:T(8,128)S(1)}, u32[]{:S(2)}, u32[]{:S(2)}) collective-permute-start(f32[9,9,8,128]{3,2,1,0:T(8,128)S(1)} %get-tuple-element.25), channel_id=1, source_target_pairs={{2,0},{4,2},{6,4},{8,6},{10,8},{12,10},{14,12},{16,14},{18,16},{20... | collective-permute-start | bytes 995336 | tf_op jit(solution)/shard_map/ppermute | solution.py:417
  45.0 0.0 collective-permute-start.3
  45.0 0.1 iota_compare_fusion
  45.0 0.1 add_convert_fusion.sel_ref
  45.1 11.4 %collective-permute-done.2.low_in = f32[9,9,8,128]{3,2,1,0:T(8,128)S(1)} collective-permute-done((f32[9,9,8,128]{3,2,1,0:T(8,128)S(1)}, f32[9,9,8,128]{3,2,1,0:T(8,128)S(1)}, u32[]{:S(2)}, u32[]{:S(2)}) %collective-permute-start.2) | collective-permute-done | bytes 331808 | tf_op jit(solution)/shard_map/ppermute | solution.py:417
  56.5 2.3 %collective-permute-done.3.high_in = f32[9,9,8,128]{3,2,1,0:T(8,128)S(1)} collective-permute-done((f32[9,9,8,128]{3,2,1,0:T(8,128)S(1)}, f32[9,9,8,128]{3,2,1,0:T(8,128)S(1)}, u32[]{:S(2)}, u32[]{:S(2)}) %collective-permute-start.3) | collective-permute-done | bytes 331808 | tf_op jit(solution)/shard_map/ppermute | solution.py:416
  58.9 9.1 %all-to-all-done = f32[32,4,128]{2,1,0:T(4,128)S(1)} async-done(((f32[32,4,128]{2,1,0:T(4,128)}), f32[32,4,128]{2,1,0:T(4,128)S(1)}, u32[]{:S(2)}, u32[]{:S(2)}) %all-to-all-start) | async-done | bytes 65568 | tf_op jit(solution)/shard_map/all_to_all | solution.py:418
  68.0 0.1 broadcast_in_dim.13.col_ref
  68.0 0.0 copy-done.6
  68.0 9.6 %third.1 = (f32[5,9,48,128]{3,2,1,0:T(8,128)S(1)}, f32[5,9,48,128]{3,2,1,0:T(8,128)S(1)}, f32[4,128]{1,0:T(4,128)S(1)}, f32[4,128]{1,0:T(4,128)S(1)}, f32[8,128]{1,0:T(8,128)S(1)}) custom-call(f32[7,7]{1,0:T(8,128)S(1)} %copy-done.6, f32[8,9,32,128]{3,2,1,0:T(8,128)S(1)} %get-tuple-element.20.f_ref, f32[8,32,128]{2,1,0:T(8,128)S(1)} %get-tuple-element.24.t8_ref, ...), custom_call_target="tpu_custom_call" | custom-call | flops 40000000 | bytes 4000000 | tf_op jit(solution)/shard_map/third/pallas_call | solution.py:421
  77.7 0.1 collective-permute-start.4
  77.8 1.1 collective-permute-done.4
  79.0 35.2 %all_to_all.15 = f32[32,4,128]{2,1,0:T(4,128)S(1)} all-to-all(f32[32,4,128]{2,1,0:T(4,128)S(1)} %broadcast_in_dim.14), channel_id=1, replica_groups=mesh['member'=4,'lon'=32,'lat'=2] {'lon'}, dimensions={0} | all-to-all | bytes 131072 | tf_op jit(solution)/shard_map/all_to_all | solution.py:431
  114.2 8.1 %fourth.1 = (f32[5,9,48,128]{3,2,1,0:T(8,128)S(1)}, f32[4,128]{1,0:T(4,128)S(1)}, f32[4,128]{1,0:T(4,128)S(1)}, f32[8,128]{1,0:T(8,128)S(1)}) custom-call(f32[7,7]{1,0:T(8,128)S(1)} %copy-done.6, f32[5,9,48,128]{3,2,1,0:T(8,128)S(1)} %get-tuple-element.28.dyn_in, f32[5,9,48,128]{3,2,1,0:T(8,128)S(1)} %get-tuple-element.29.stat_in_ref, ...), custom_call_target="tpu_custom_call" | custom-call | flops 30000000 | bytes 4000000 | tf_op jit(solution)/shard_map/fourth/pallas_call | solution.py:434
  122.3 0.1 collective-permute-start.5
  122.4 1.1 collective-permute-done.5
  123.6 29.6 %all_to_all.16 = f32[32,4,128]{2,1,0:T(4,128)S(1)} all-to-all(f32[32,4,128]{2,1,0:T(4,128)S(1)} %broadcast_in_dim.15), channel_id=1, replica_groups=mesh['member'=4,'lon'=32,'lat'=2] {'lon'}, dimensions={0} | all-to-all | bytes 131072 | tf_op jit(solution)/shard_map/all_to_all | solution.py:431
  153.2 5.2 %fifth.1 = (f32[3,32,1080]{2,1,0:T(8,128)}, f32[32,1080]{1,0:T(8,128)}, f32[3]{0:T(128)}) custom-call(f32[7,7]{1,0:T(8,128)S(1)} %copy-done.6, f32[5,9,48,128]{3,2,1,0:T(8,128)S(1)} %get-tuple-element.33.dyn_in, f32[5,9,48,128]{3,2,1,0:T(8,128)S(1)} %get-tuple-element.29.stat_in_ref, f32[128,128]{1,0:T(8,128)S(1)} %bitcast.6, ...), custom_call_target="tpu_custom_call" | custom-call | flops 20000000 | bytes 4000000 | tf_op jit(solution)/shard_map/fifth/pallas_call | solution.py:441
  (8 shorter events, 0.1 us)
Async XLA Ops:
  0.6 7.1 %copy-start = (s32[1024]{0:T(1024)S(1)}, s32[1024]{0:T(1024)}, u32[]{:S(2)}) copy-start(s32[1024]{0:T(1024)} %param.12) | copy-start | bytes 12292
  0.6 1.0 copy-start.1
  1.7 1.0 copy-start.2
  2.7 0.9 copy-start.3
  3.6 0.9 copy-start.4
  4.5 0.9 copy-start.5
  7.0 61.0 %copy-start.6 = (f32[7,7]{1,0:T(8,128)S(1)}, f32[7,7]{1,0:T(8,128)}, u32[]{:S(2)}) copy-start(f32[7,7]{1,0:T(8,128)} %w_ref.5) | copy-start | bytes 592
  7.1 1.4 collective-permute-start.1
  7.2 1.5 collective-permute-start
  9.4 58.6 %all-to-all-start = ((f32[32,4,128]{2,1,0:T(4,128)}), f32[32,4,128]{2,1,0:T(4,128)S(1)}, u32[]{:S(2)}, u32[]{:S(2)}) async-start(f32[32,4,128]{2,1,0:T(4,128)} %get-tuple-element.27), calls=%async_computation | async-start | bytes 131072 | tf_op jit(solution)/shard_map/all_to_all | solution.py:418
  42.0 14.5 %collective-permute-start.2 = (f32[9,9,8,128]{3,2,1,0:T(8,128)S(1)}, f32[9,9,8,128]{3,2,1,0:T(8,128)S(1)}, u32[]{:S(2)}, u32[]{:S(2)}) collective-permute-start(f32[9,9,8,128]{3,2,1,0:T(8,128)S(1)} %get-tuple-element.25), channel_id=1, source_target_pairs={{2,0},{4,2},{6,4},{8,6},{10,8},{12,10},{14,12},{16,14},{18,16},{20... | collective-permute-start | bytes 995336 | tf_op jit(solution)/shard_map/ppermute | solution.py:417
  45.0 13.9 %collective-permute-start.3 = (f32[9,9,8,128]{3,2,1,0:T(8,128)S(1)}, f32[9,9,8,128]{3,2,1,0:T(8,128)S(1)}, u32[]{:S(2)}, u32[]{:S(2)}) collective-permute-start(f32[9,9,8,128]{3,2,1,0:T(8,128)S(1)} %get-tuple-element.26), channel_id=1, source_target_pairs={{0,2},{2,4},{4,6},{6,8},{8,10},{10,12},{12,14},{14,16},{16,18},{18... | collective-permute-start | bytes 995336 | tf_op jit(solution)/shard_map/ppermute | solution.py:416
  77.7 1.3 collective-permute-start.4
  122.3 1.3 collective-permute-start.5

commit v3 on v2

v3 whole, which is shorter than its diff:
```python
import functools
import jax
import jax.numpy as jnp
from jax import lax
from jax.experimental import pallas as pl
from jax.experimental.pallas import tpu as pltpu
from jax.sharding import PartitionSpec as P


ITERS = 3
HALO = 9
LANES = 128
PAD = 16
F32 = jnp.float32
VM = pl.BlockSpec(memory_space=pltpu.VMEM)
SM = pl.BlockSpec(memory_space=pltpu.SMEM)


def small():
    return pltpu.CompilerParams(vmem_limit_bytes=12 * 1024 * 1024)


def is_north():
    return lax.axis_index("lat") == lax.axis_size("lat") - 1


def cost(flops, size):
    return pl.CostEstimate(flops=flops, bytes_accessed=size, transcendentals=0)


def overstress(e, rc):
    half = (e[0] - e[1]) * 0.5
    tau = jnp.sqrt(half * half + e[2] * e[2] + 0.25)
    over = jnp.maximum((tau + 0.35 * (e[0] + e[1])) * rc, 1.0)
    return over - 1.0, 1.0 - 1.0 / over


def physics(damage, stress, bl, rc):
    keep = 1.0 - damage
    k2 = keep * keep
    g = k2 / (k2 + 0.5)
    e = [g * (stress[k] + keep * bl[k]) for k in range(3)]
    excess, q = overstress(e, rc)
    return e, q, excess


def tops(tiles, single, at):
    t = jnp.concatenate(tiles, axis=0).T
    rows = [t[at - k : at - k + 1, :] for k in range(3)]
    parts = [single] + [pltpu.roll(single, k, 1) for k in (1, 2)] + [jnp.zeros_like(single)]
    return rows + [jnp.concatenate(parts, axis=0).T[at : at + 1, :]]


def total(x):
    return jnp.sum(jnp.sum(x, axis=0, keepdims=True), axis=1, keepdims=True)


def first_kernel(nrows, *refs):
    given, (f_ref, lat_out, chunk_ref, sum_ref), held, sem = refs[:5], refs[5:9], refs[9:14], refs[14]
    copies = [pltpu.make_async_copy(a, b, sem.at[n]) for n, (a, b) in enumerate(zip(given, held, strict=True))]
    for n in (2, 4, 3, 0, 1):
        copies[n].start()
    strain, stress, conc, cls, mask = held
    nt = f_ref.shape[1]
    ncols = conc.shape[0]
    f_ref[:, nt - 1] = jnp.zeros((8, ncols, LANES), F32)
    parts = [(c, min(LANES, nrows - c * LANES), slice(c * LANES, min(nrows, (c + 1) * LANES))) for c in range(nt)]
    for n in (2, 4, 3):
        copies[n].wait()
    for c, w, sl in parts:
        con = conc[:, sl]
        oc = mask[:, sl].astype(F32)
        f_ref[0, c, :, 0:w] = oc * con * jnp.exp(-2.0 * (1.0 - con))
        f_ref[6, c, :, 0:w] = oc * con
        f_ref[7, c, :, 0:w] = oc * 0.1 * cls[:, sl].astype(F32) * con
    copies[0].wait()
    third = 1.0 / 3.0
    for c, w, sl in parts:
        e1, e2, e3 = (strain[k, :, sl] for k in range(3))
        base = f_ref[0, c, :, 0:w]
        f_ref[0, c, :, 0:w] = base * ((e1 + e2 * third) * 1.125)
        f_ref[1, c, :, 0:w] = base * ((e2 + e1 * third) * 1.125)
        f_ref[2, c, :, 0:w] = base * (e3 * (0.75 * 1.125))
    copies[1].wait()
    for c, w, sl in parts:
        oc = jnp.where(f_ref[6, c, :, 0:w] > 0.0, 1.0, 0.0)
        for k in range(3):
            f_ref[3 + k, c, :, 0:w] = oc * stress[k, :, sl]
    excess = jnp.zeros((ncols, LANES), F32)
    count = jnp.zeros((ncols, LANES), F32)
    for c in range(nt):
        d, mc, e, _, over, oc, _ = start_state([f_ref[k, c] for k in range(8)])
        excess = excess + over
        count = count + oc
    at = nrows - 1 - (nt - 1) * LANES
    rows = tops([d, mc, e[0], e[1]], e[2], at)
    s = total(excess)
    n = total(count)
    lane1 = lax.broadcasted_iota(jnp.int32, (1, LANES), 1)
    sums = jnp.where(lane1 == 96, s, 0.0) + jnp.where(lane1 == 97, n, 0.0)
    for k, row in enumerate(rows):
        chunk_ref[k : k + 1, :] = row
    sum_ref[...] = jnp.broadcast_to(sums, sum_ref.shape)
    north = is_north()
    for f in range(8):
        lat_out[f] = jnp.where(north, f_ref[f, 0], f_ref[f, nt - 1])


def start_state(vals):
    bl, st, mc, d = vals[0:3], vals[3:6], vals[6], vals[7]
    oc = jnp.where(mc > 0.0, 1.0, 0.0)
    rc = oc / (0.6 * jnp.where(mc > 0.0, mc, 1.0))
    e, q, over = physics(d, st, bl, rc)
    return d, mc, e, q, over, oc, rc


def second_kernel(nrows, f_ref, lat_in, chunk_ref, sum_ref, sum_in, t8_ref, low_ref, high_ref, send_ref):
    nt = f_ref.shape[1]
    ncols = f_ref.shape[2]
    edge = nrows - (nt - 1) * LANES
    lane = lax.broadcasted_iota(jnp.int32, (ncols, LANES), 1)
    north = is_north()
    own = lane < edge
    keep = jnp.where(north, (lane >= LANES - HALO).astype(jnp.int32), ((lane >= edge) & (lane < edge + HALO)).astype(jnp.int32)) > 0
    for f in range(8):
        got = jnp.where(north, pltpu.roll(lat_in[f], (LANES - edge) % LANES, 1), pltpu.roll(lat_in[f], edge, 1))
        t8_ref[f] = jnp.where(own, f_ref[f, nt - 1], jnp.where(keep, got, 0.0))
    for f in range(8):
        for c in range(nt):
            at = t8_ref.at[f] if c == nt - 1 else f_ref.at[f, c]
            low_ref[f, c] = at[0:8]
            low_ref[8, c, f : f + 1] = at[8:9]
            high_ref[f, c] = at[ncols - 8 : ncols]
            high_ref[8, c, f : f + 1] = at[ncols - 9 : ncols - 8]
    s = sum_ref[0:1, :] + sum_in[0:1, :]
    chunk = [chunk_ref[k : k + 1, :] for k in range(4)]
    chunk[3] = chunk[3] + s
    block = jnp.concatenate(chunk, axis=0)
    for n in range(send_ref.shape[0]):
        send_ref[n] = block


def ghosts(got_ref, sel_ref, col_ref):
    n = got_ref.shape[0] // 4
    parts = []
    for r in range(4):
        m = got_ref[pl.ds(r, n, stride=4), :]
        h = m.astype(jnp.bfloat16)
        m = m - h.astype(F32)
        h2 = m.astype(jnp.bfloat16)
        h3 = (m - h2.astype(F32)).astype(jnp.bfloat16)
        parts.append(jnp.concatenate([h, h2, h3], axis=0))
    picked = jnp.dot(sel_ref[...], jnp.concatenate(parts, axis=1), preferred_element_type=F32)
    lane = lax.broadcasted_iota(jnp.int32, (sel_ref.shape[0], LANES), 1)
    col = col_ref[...] == (lane & 31)
    group = lane >> 5
    picked = [jnp.where(col, picked[:, r * LANES : (r + 1) * LANES], 0.0) for r in range(4)]
    out = []
    for f in range(5):
        vals = []
        for k in range(3):
            row, g = (k, f) if f < 4 else (3, k)
            vals.append(jnp.sum(jnp.where(group == g, picked[row], 0.0), axis=1, keepdims=True))
        out.append(vals)
    return out


def smooth_into(w_ref, g_ref, acc_ref, nf, start, tiles):
    nt = g_ref.shape[1]
    lane = lax.broadcasted_iota(jnp.int32, (8, LANES), 1)

    def one(f, i):
        row = start + i * 8
        mid, rolled = {}, {}
        for c in range(nt):
            x = [g_ref[f, c, pl.ds(row + a - 3, 8), :] for a in range(7)]
            for b in range(7):
                t = w_ref[0, b] * x[0]
                for a in range(1, 7):
                    t = t + w_ref[a, b] * x[a]
                if b == 3:
                    mid[c] = t
                else:
                    rolled[c, b] = pltpu.roll(t, (3 - b) % LANES, 1)
        for c in range(nt):
            t = mid[c]
            for b in range(3):
                t = t + (jnp.where(lane < 3 - b, rolled[(c - 1) % nt, b], rolled[c, b]) if nt > 1 else rolled[c, b])
            for b in range(4, 7):
                t = t + (jnp.where(lane >= LANES - (b - 3), rolled[(c + 1) % nt, b], rolled[c, b]) if nt > 1 else rolled[c, b])
            acc_ref[f, c, pl.ds(pl.multiple_of(i * 8, 8), 8), :] = t

    def body(step, _):
        one(step // tiles, step % tiles)
        return 0

    lax.fori_loop(0, nf * tiles, body, 0)


def lane_value(row, at):
    lane1 = lax.broadcasted_iota(jnp.int32, row.shape, 1)
    return jnp.sum(jnp.where(lane1 == at, row, 0.0), axis=1, keepdims=True)


def received_sums(got_ref):
    return jnp.sum(got_ref[pl.ds(3, got_ref.shape[0] // 4, stride=4), :], axis=0, keepdims=True)


def ghost_sums(w_ref, got_ref, sel_ref, col_ref, gg_ref, ga_ref, factor, edge, first, start, tiles):
    gh = ghosts(got_ref, sel_ref, col_ref)
    d, q = gh[0], gh[1]
    if first:
        oc = [jnp.where(v > 0.0, 1.0, 0.0) for v in q]
        rc = [1.0 / (0.6 * jnp.where(v > 0.0, v, 1.0)) for v in q]
        q = [oc[k] * overstress([gh[2 + m][k] for m in range(3)], rc[k])[1] for k in range(3)]
    vals = [[d[k] + factor * (1.0 - d[k]) * q[k] for k in range(3)]]
    for m in range(3):
        vals.append([gh[2 + m][k] * (1.0 - factor * q[k]) for k in range(3)])
    if first:
        vals.append(oc)
    shape = gg_ref.shape[2:]
    lane = lax.broadcasted_iota(jnp.int32, shape, 1)
    at = jnp.where(is_north(), edge, -4)
    for f, v in enumerate(vals):
        t = jnp.zeros(shape, F32)
        for k in range(3):
            t = jnp.where(lane == at + k, v[k], t)
        gg_ref[f, 0] = t
    smooth_into(w_ref, gg_ref, ga_ref, len(vals), start, tiles)


def coefficients(r, g, acc):
    x = [0.5 * g[0] + r * acc[0]] + [0.5 * g[2 + k] + r * acc[2 + k] for k in range(3)]
    y = [0.5 * g[1] + r * acc[1]] + [-(0.5 * g[5 + k] + r * acc[5 + k]) for k in range(3)]
    return x, y


def put_parts(g_ref, c, at, d, q, e):
    g_ref[0, c, at, :] = d
    g_ref[1, c, at, :] = (1.0 - d) * q
    for k in range(3):
        g_ref[2 + k, c, at, :] = e[k]
        g_ref[5 + k, c, at, :] = e[k] * q


def ahead_first(w_ref, f_ref, t8_ref, low_in, high_in, x_ref, y_ref, stat_ref, r_ref, edge_ref, g_ref, acc_ref):
    nt = f_ref.shape[1]
    ncols = f_ref.shape[2]
    n = x_ref.shape[2]

    def local(vals, c, row, nr):
        d, _, e, q, _, oc, rc = start_state(vals)
        at = slice(row, row + nr)
        put_parts(g_ref, c, at, d, q, e)
        g_ref[8, c, at, :] = oc
        if nr == 8:
            to = slice(row - 8, row)
            for k in range(3):
                stat_ref[k, c, to, :] = vals[k]
            stat_ref[3, c, to, :] = rc

    for c in range(nt):
        local([high_in[8, c, f : f + 1, :] for f in range(8)], c, PAD - 9, 1)
        local([high_in[f, c] for f in range(8)], c, PAD - 8, 8)
        for i in range(ncols // 8):
            at = slice(8 * i, 8 * i + 8)
            local([(t8_ref[f, at, :] if c == nt - 1 else f_ref[f, c, at, :]) for f in range(8)], c, PAD + 8 * i, 8)
        local([low_in[f, c] for f in range(8)], c, PAD + ncols, 8)
        local([low_in[8, c, f : f + 1, :] for f in range(8)], c, PAD + ncols + 8, 1)
    smooth_into(w_ref, g_ref, acc_ref, 9, 8, n // 8)
    for i in range(n // 8):
        at, to = slice(8 + 8 * i, 16 + 8 * i), slice(8 * i, 8 * i + 8)
        for c in range(nt - 1):
            r = 0.5 * g_ref[8, c, at, :] / (acc_ref[8, c, to, :] + 1.0)
            r_ref[c, to, :] = r
            x, y = coefficients(r, [g_ref[f, c, at, :] for f in range(8)], [acc_ref[f, c, to, :] for f in range(8)])
            for f in range(4):
                x_ref[f, c, to, :] = x[f]
                y_ref[f, c, to, :] = y[f]
        for f in range(9):
            edge_ref[f, to, :] = g_ref[f, nt - 1, at, :]
            edge_ref[9 + f, to, :] = acc_ref[f, nt - 1, to, :]


def ahead_later(skip, w_ref, dyn_in, r_ref, r8_ref, x_ref, y_ref, g_ref, acc_ref):
    nt = dyn_in.shape[1]
    n = x_ref.shape[2]
    for i in range(dyn_in.shape[2] // 8):
        at = slice(8 * i, 8 * i + 8)
        for c in range(nt):
            put_parts(g_ref, c, at, *[dyn_in[f, c, at, :] for f in range(2)], [dyn_in[2 + k, c, at, :] for k in range(3)])
    smooth_into(w_ref, g_ref, acc_ref, 8, 4, n // 8)
    for i in range(n // 8):
        at, to, fr = slice(4 + 8 * i, 12 + 8 * i), slice(8 * i, 8 * i + 8), slice(skip + 8 * i, skip + 8 * i + 8)
        for c in range(nt):
            r = r8_ref[fr, :] if c == nt - 1 else r_ref[c, fr, :]
            x, y = coefficients(r, [g_ref[f, c, at, :] for f in range(8)], [acc_ref[f, c, to, :] for f in range(8)])
            for f in range(4):
                x_ref[f, c, to, :] = x[f]
                y_ref[f, c, to, :] = y[f]


def next_state(c, at, to, new, stat_ref, dyn_ref):
    e, q, over = physics(new[0], new[1:], [stat_ref[k, c, at, :] for k in range(3)], stat_ref[3, c, at, :])
    dyn_ref[0, c, to, :] = new[0]
    dyn_ref[1, c, to, :] = q
    for k in range(3):
        dyn_ref[2 + k, c, to, :] = e[k]
    return over


def send_next(dyn_ref, own, excess, edge, chunk_ref, sum_ref):
    nt = dyn_ref.shape[1]
    tile = [dyn_ref[f, nt - 1, own, :] for f in range(5)]
    rows = tops(tile[:4], tile[4], edge - 1)
    s = total(excess)
    lane1 = lax.broadcasted_iota(jnp.int32, (1, LANES), 1)
    sums = jnp.where(lane1 == 96, s, 0.0)
    rows[3] = rows[3] + sums
    for k, row in enumerate(rows):
        chunk_ref[k : k + 1, :] = row
    zero = jnp.zeros((1, LANES), F32)
    for k in range(4):
        sum_ref[k : k + 1, :] = sums if k == 3 else zero


def after_first(
    nrows, ncols, w_ref, x_ref, y_ref, stat_ref, edge_ref, got_ref, sel_ref, col_ref,
    dyn_ref, r8_ref, chunk_ref, sum_ref, mean_ref, gg_ref, ga_ref,
):
    nt = x_ref.shape[1] + 1
    n = x_ref.shape[2]
    edge = nrows - (nt - 1) * LANES
    sums = received_sums(got_ref)
    count = lane_value(sums, 97) + 1.0
    mean = lane_value(sums, 96) / count
    factor = 1.0 / (1.0 + 2.0 * mean)
    lane1 = lax.broadcasted_iota(jnp.int32, mean_ref.shape, 1)
    mean_ref[...] = jnp.where(lane1 == 1, mean, count)
    lane = lax.broadcasted_iota(jnp.int32, (8, LANES), 1)
    f8 = jnp.broadcast_to(factor, (8, LANES))
    ghost_sums(w_ref, got_ref, sel_ref, col_ref, gg_ref, ga_ref, factor, edge, True, 8, n // 8)
    excess = jnp.zeros((8, LANES), F32)
    for i in range(n // 8):
        at = slice(8 * i, 8 * i + 8)
        own = PAD - 8 <= 8 * i < PAD - 8 + ncols
        for c in range(nt):
            if c == nt - 1:
                r = 0.5 * edge_ref[8, at, :] / (edge_ref[17, at, :] + ga_ref[4, 0, at, :] + 1.0)
                r8_ref[at, :] = r
                x, y = coefficients(r, [edge_ref[f, at, :] for f in range(8)], [edge_ref[9 + f, at, :] for f in range(8)])
                new = [x[f] + f8 * y[f] + r * ga_ref[f, 0, at, :] for f in range(4)]
            else:
                new = [x_ref[f, c, at, :] + f8 * y_ref[f, c, at, :] for f in range(4)]
            over = next_state(c, at, at, new, stat_ref, dyn_ref)
            if own:
                excess = excess + (jnp.where(lane < edge, over, 0.0) if c == nt - 1 else over)
    send_next(dyn_ref, slice(PAD - 8, PAD - 8 + ncols), excess, edge, chunk_ref, sum_ref)


def after_second(
    nrows, ncols, w_ref, x_ref, y_ref, stat_ref, r8_ref, got_ref, sel_ref, col_ref, mean_in,
    dyn_ref, chunk_ref, sum_ref, mean_ref, gg_ref, ga_ref,
):
    nt = x_ref.shape[1]
    n = x_ref.shape[2]
    edge = nrows - (nt - 1) * LANES
    mean = lane_value(received_sums(got_ref), 96) / lane_value(mean_in[0:1, :], 0)
    factor = 1.0 / (1.0 + 2.0 * mean)
    lane1 = lax.broadcasted_iota(jnp.int32, mean_ref.shape, 1)
    mean_ref[...] = jnp.where(lane1 == 2, mean, mean_in[...])
    lane = lax.broadcasted_iota(jnp.int32, (8, LANES), 1)
    row = lax.broadcasted_iota(jnp.int32, (8, LANES), 0)
    f8 = jnp.broadcast_to(factor, (8, LANES))
    ghost_sums(w_ref, got_ref, sel_ref, col_ref, gg_ref, ga_ref, factor, edge, False, 12, n // 8)
    excess = jnp.zeros((8, LANES), F32)
    for i in range(n // 8):
        at, to = slice(4 + 8 * i, 12 + 8 * i), slice(8 * i, 8 * i + 8)
        for c in range(nt):
            new = [x_ref[f, c, to, :] + f8 * y_ref[f, c, to, :] for f in range(4)]
            if c == nt - 1:
                new = [new[f] + r8_ref[at, :] * ga_ref[f, 0, to, :] for f in range(4)]
            over = next_state(c, at, to, new, stat_ref, dyn_ref)
            if 8 * i < 4:
                over = jnp.where(row >= 4, over, 0.0)
            if 8 * i + 8 > 4 + ncols:
                over = jnp.where(row < 4, over, 0.0)
            excess = excess + (jnp.where(lane < edge, over, 0.0) if c == nt - 1 else over)
    send_next(dyn_ref, slice(4, 4 + ncols), excess, edge, chunk_ref, sum_ref)


def after_third(
    nrows, ncols, w_ref, x_ref, y_ref, r8_ref, got_ref, sel_ref, col_ref, mean_in,
    stress_ref, damage_ref, mean_ref, gg_ref, ga_ref,
):
    nt = x_ref.shape[1]
    edge = nrows - (nt - 1) * LANES
    row = mean_in[0:1, :]
    mean = lane_value(received_sums(got_ref), 96) / lane_value(row, 0)
    factor = 1.0 / (1.0 + 2.0 * mean)
    for at, one in enumerate((lane_value(row, 1), lane_value(row, 2), mean)):
        mean_ref[at] = jnp.sum(one)
    f8 = jnp.broadcast_to(factor, (8, LANES))
    ghost_sums(w_ref, got_ref, sel_ref, col_ref, gg_ref, ga_ref, factor, edge, False, PAD, ncols // 8)
    for c in range(nt):
        w = min(LANES, nrows - c * LANES)
        for i in range(ncols // 8):
            at = slice(8 * i, 8 * i + 8)
            for f in range(4):
                v = x_ref[f, c, at, :] + f8 * y_ref[f, c, at, :]
                if c == nt - 1:
                    v = v + r8_ref[8 + 8 * i : 16 + 8 * i, :] * ga_ref[f, 0, at, :]
                if f == 0:
                    damage_ref[at, c * LANES : c * LANES + w] = v[:, 0:w]
                else:
                    stress_ref[f - 1, at, c * LANES : c * LANES + w] = v[:, 0:w]


def step(strain_rate, stress_start, concentration, cell_class, land_mask, fold_partner, kernel_weights):
    ncols, nrows = concentration.shape
    nt = -(-nrows // LANES)
    nlon = lax.axis_size("lon")
    nlat = lax.axis_size("lat")
    rows = ncols + 2 * PAD
    n1, n2 = rows - 16, rows - 24
    sds = lambda *s: jax.ShapeDtypeStruct(s, F32)
    vmem = lambda *s: pltpu.VMEM(s, F32)

    def call(body, flops, *args, weights=True, **kw):
        given = args if not weights else (kernel_weights, *args)
        return pl.pallas_call(
            body, in_specs=([SM] if weights else []) + [VM] * len(args), cost_estimate=cost(flops, flops),
            compiler_params=small(), **kw,
        )(*given)

    columns = (lax.axis_index("lon") * ncols - PAD + jnp.arange(rows, dtype=jnp.int32)) % (ncols * nlon)
    partner = jnp.take(fold_partner, columns)
    sel = (partner[:, None] // ncols == jnp.arange(nlon)[None, :]).astype(jnp.bfloat16)
    sel = jnp.concatenate([sel, sel, sel], axis=1)
    col = jnp.broadcast_to((partner % ncols)[:, None], (rows, LANES)).astype(jnp.int32)

    given = (strain_rate, stress_start, concentration, cell_class, land_mask)
    f, lat_out, chunk, sums = pl.pallas_call(
        functools.partial(first_kernel, nrows),
        out_shape=(sds(8, nt, ncols, LANES), sds(8, ncols, LANES), sds(4, LANES), sds(8, LANES)),
        in_specs=[pl.BlockSpec(memory_space=pltpu.HBM)] * 5, out_specs=(VM,) * 4,
        scratch_shapes=[pltpu.VMEM(a.shape, a.dtype) for a in given] + [pltpu.SemaphoreType.DMA((5,))],
        cost_estimate=cost(4000000, 2000000), compiler_params=small(), name="first",
    )(*(pltpu.with_memory_space_constraint(a, pltpu.HBM) for a in given))
    swap = [(i, nlat - 1 - i) for i in range(nlat)]
    lat_in = lax.ppermute(lat_out, "lat", swap)
    sum_in = lax.ppermute(sums, "lat", swap)
    t8, low, high, send = call(
        functools.partial(second_kernel, nrows), 400000, f, lat_in, chunk, sums, sum_in, weights=False,
        out_shape=(sds(8, ncols, LANES), sds(9, nt, 8, LANES), sds(9, nt, 8, LANES), sds(nlon, 4, LANES)), out_specs=(VM,) * 4,
    )
    up = [(i, (i + 1) % nlon) for i in range(nlon)]
    down = [(j, i) for i, j in up]
    high_in = lax.ppermute(high, "lon", up)
    low_in = lax.ppermute(low, "lon", down)
    got = lax.all_to_all(send, "lon", 0, 0, tiled=True).reshape(nlon * 4, LANES)

    x, y, stat, r, edge = call(
        ahead_first, 60000000, f, t8, low_in, high_in,
        out_shape=(sds(4, nt - 1, n1, LANES), sds(4, nt - 1, n1, LANES), sds(4, nt, n1, LANES), sds(nt - 1, n1, LANES), sds(18, n1, LANES)),
        out_specs=(VM,) * 5, scratch_shapes=[vmem(9, nt, rows, LANES), vmem(9, nt, n1, LANES)],
    )
    dyn, r8, chunk, sums, mean = call(
        functools.partial(after_first, nrows, ncols), 4000000, x, y, stat, edge, got, sel, col,
        out_shape=(sds(5, nt, n1, LANES), sds(n1, LANES), sds(4, LANES), sds(4, LANES), sds(8, LANES)),
        out_specs=(VM,) * 5, scratch_shapes=[vmem(5, 1, rows, LANES), vmem(5, 1, n1, LANES)],
    )

    def spread(chunk, sums):
        chunk = chunk + lax.ppermute(sums, "lat", swap)
        send = jnp.broadcast_to(chunk[None], (nlon, 4, LANES))
        return lax.all_to_all(send, "lon", 0, 0, tiled=True).reshape(nlon * 4, LANES)

    got = spread(chunk, sums)
    x, y = call(
        functools.partial(ahead_later, 4), 50000000, dyn, r, r8,
        out_shape=(sds(4, nt, n2, LANES), sds(4, nt, n2, LANES)), out_specs=(VM,) * 2,
        scratch_shapes=[vmem(8, nt, n1, LANES), vmem(8, nt, n2, LANES)],
    )
    dyn, chunk, sums, mean = call(
        functools.partial(after_second, nrows, ncols), 4000000, x, y, stat, r8, got, sel, col, mean,
        out_shape=(sds(5, nt, n2, LANES), sds(4, LANES), sds(4, LANES), sds(8, LANES)),
        out_specs=(VM,) * 4, scratch_shapes=[vmem(4, 1, rows, LANES), vmem(4, 1, n2, LANES)],
    )
    got = spread(chunk, sums)
    x, y = call(
        functools.partial(ahead_later, 8), 40000000, dyn, r, r8,
        out_shape=(sds(4, nt, ncols, LANES), sds(4, nt, ncols, LANES)), out_specs=(VM,) * 2,
        scratch_shapes=[vmem(8, nt, n2, LANES), vmem(8, nt, ncols, LANES)],
    )
    return call(
        functools.partial(after_third, nrows, ncols), 4000000, x, y, r8, got, sel, col, mean,
        out_shape=(sds(3, ncols, nrows), sds(ncols, nrows), sds(ITERS)), out_specs=(VM, VM, SM),
        scratch_shapes=[vmem(4, 1, rows, LANES), vmem(4, 1, ncols, LANES)],
    )


def solution(mesh):
    in_specs = (
        P(None, "lon", "lat"),
        P(None, "lon", "lat"),
        P("lon", "lat"),
        P(("member", "lon"), "lat"),
        P("lon", "lat"),
        P(),
        P(),
    )
    out_specs = (P(None, ("member", "lon"), "lat"), P(("member", "lon"), "lat"), P("member"))
    return jax.shard_map(step, mesh=mesh, in_specs=in_specs, out_specs=out_specs, check_vma=False)
```

time: 159 us -> 162 us (1.019)
  blocking collectives: 64.9 us -> 0 us
  waiting for transfers between devices: 25.3 us -> 51.1 us
  starting transfers between devices: 36.5 us -> 61 us
  Pallas kernels: 25.2 us -> 39.2 us
  local copies, waits for them, and re-layouts: 5.6 us -> 8.38 us
    all_to_all x2 -> x0, blocking collectives: 64.9 us -> none  [spread(): lax.all_to_all(send, 'lon', 0, 0, tiled=True).reshape(nlon * 4, LANES)]
    all_to_all x1 -> x3, waiting for transfers between devices: 9.1 us -> 35.5 us  [the longest x2 35.5 us: spread(): lax.all_to_all(send, 'lon', 0, 0, tiled=True).reshape(nlon * 4, LANES)]
    all_to_all x1 -> x3, starting transfers between devices: 32.7 us -> 57.2 us  [the longest x1 32.7 us: step(): got = lax.all_to_all(send, 'lon', 0, 0, tiled=True).reshape(nlon * 4, LANES)]
    pallas_call x5 -> x8, Pallas kernels: 25.2 us -> 39.2 us  [the longest x7 37.4 us: call(): pl.pallas_call(body, in_specs=([SM] if weights else []) + [VM] * len(args...]
    unnamed x14 -> x20, local copies, waits for them, and re-layouts: 4.77 us -> 6.29 us
  transfers between devices with their start and end apart: 7 -> 9, of which waited for: 6 -> 7; matrix products, arithmetic and copies ran while one was open for 1% -> 1% of each run, Pallas kernels for 0% -> 16%
where the time goes in v3:
time: 162 us; the launch traced here: 161 us
  starting transfers between devices  61 us (38%)
  waiting for transfers between devices  51.1 us (32%)
  Pallas kernels  39.2 us (24%)
  local copies, waits for them, and re-layouts  8.38 us (5%)
    pallas_call x7, Pallas kernels, call(): pl.pallas_call(body, in_specs=([SM] if weights else []) + [VM] * len(args...  37.4 us
    all_to_all x2, waiting for transfers between devices, spread(): lax.all_to_all(send, 'lon', 0, 0, tiled=True).reshape(nlon * 4, LANES)  35.5 us
    all_to_all x1, starting transfers between devices, step(): got = lax.all_to_all(send, 'lon', 0, 0, tiled=True).reshape(nlon * 4, LANES)  32.7 us
    all_to_all x2, starting transfers between devices, spread(): lax.all_to_all(send, 'lon', 0, 0, tiled=True).reshape(nlon * 4, LANES)  24.5 us
    ppermute x1, waiting for transfers between devices, step(): low_in = lax.ppermute(low, 'lon', down)  10.8 us
    unnamed x20, local copies, waits for them, and re-layouts  6.29 us
  transfers between devices with their start and end apart: 9, of which 7 were waited for; matrix products, arithmetic and copies ran while one was open for 1% of the time, Pallas kernels for 16%

profile of v3, /device:TPU:38, one launch (start us, length us, event | category | flops | bytes accessed | tf_op | source)
XLA Modules:
  0.0 161.2 jit_solution(12284207533774134014)
XLA Ops:
  0.6 0.0 copy-start
  0.6 1.8 %first.1 = (f32[8,9,32,128]{3,2,1,0:T(8,128)S(1)}, f32[8,32,128]{2,1,0:T(8,128)S(1)}, f32[4,128]{1,0:T(4,128)S(1)}, f32[8,128]{1,0:T(8,128)S(1)}) custom-call(f32[3,32,1080]{2,1,0:T(8,128)} %refs_0_.1, f32[3,32,1080]{2,1,0:T(8,128)} %refs_1_.1, f32[32,1080]{1,0:T(8,128)} %refs_2_.1, s32[32,1080]{1,0:T(8,128)} %refs_3_.1, s32[32,1080]{1,0:T(8,128)} %refs_4_.1), custom_call_target="tpu_custom_call" | custom-call | flops 4000000 | bytes 2000000 | tf_op jit(solution)/shard_map/first/pallas_call | solution.py:443
  2.4 0.0 copy-start.7
  2.5 0.1 collective-permute-start.1
  2.6 0.5 collective-permute-start
  3.1 0.0 copy-done
  3.1 0.7 gather_fusion
  3.9 0.0 collective-permute-done.1.sum_in
  3.9 0.2 collective-permute-done.lat_in
  4.1 0.7 shard_map.94
  4.8 0.0 copy-start.8
  4.8 0.7 copy-done.8
  5.4 32.7 %all-to-all-start = ((f32[32,4,128]{2,1,0:T(4,128)}), f32[32,4,128]{2,1,0:T(4,128)}, u32[]{:S(2)}, u32[]{:S(2)}) async-start(f32[32,4,128]{2,1,0:T(4,128)} %get-tuple-element.40), calls=%async_computation | async-start | bytes 131072 | tf_op jit(solution)/shard_map/all_to_all | solution.py:461
  38.1 2.9 %collective-permute-start.2 = (f32[9,9,8,128]{3,2,1,0:T(8,128)S(1)}, f32[9,9,8,128]{3,2,1,0:T(8,128)S(1)}, u32[]{:S(2)}, u32[]{:S(2)}) collective-permute-start(f32[9,9,8,128]{3,2,1,0:T(8,128)S(1)} %get-tuple-element.34), channel_id=1, source_target_pairs={{2,0},{4,2},{6,4},{8,6},{10,8},{12,10},{14,12},{16,14},{18,16},{20... | collective-permute-start | bytes 995336 | tf_op jit(solution)/shard_map/ppermute | solution.py:460
  41.0 0.0 collective-permute-start.3
  41.0 0.1 iota_compare_fusion
  41.1 0.7 add_convert_fusion.sel_ref
  41.8 10.8 %collective-permute-done.2.low_in = f32[9,9,8,128]{3,2,1,0:T(8,128)S(1)} collective-permute-done((f32[9,9,8,128]{3,2,1,0:T(8,128)S(1)}, f32[9,9,8,128]{3,2,1,0:T(8,128)S(1)}, u32[]{:S(2)}, u32[]{:S(2)}) %collective-permute-start.2) | collective-permute-done | bytes 331808 | tf_op jit(solution)/shard_map/ppermute | solution.py:460
  52.6 2.3 %collective-permute-done.3.high_in = f32[9,9,8,128]{3,2,1,0:T(8,128)S(1)} collective-permute-done((f32[9,9,8,128]{3,2,1,0:T(8,128)S(1)}, f32[9,9,8,128]{3,2,1,0:T(8,128)S(1)}, u32[]{:S(2)}, u32[]{:S(2)}) %collective-permute-start.3) | collective-permute-done | bytes 331808 | tf_op jit(solution)/shard_map/ppermute | solution.py:459
  54.9 0.0 copy-done.7
  54.9 0.9 copy-done.9
  55.8 11.2 %shard_map.95 = (f32[4,8,48,128]{3,2,1,0:T(8,128)S(1)}, f32[4,8,48,128]{3,2,1,0:T(8,128)S(1)}, f32[4,9,48,128]{3,2,1,0:T(8,128)S(1)}, f32[8,48,128]{2,1,0:T(8,128)S(1)}, f32[18,48,128]{2,1,0:T(8,128)S(1)}) custom-call(f32[7,7]{1,0:T(8,128)S(1)} %copy-done.7, f32[8,9,32,128]{3,2,1,0:T(8,128)S(1)} %get-tuple-element.29.f_ref, f32[8,32,128]{2,1,0:T(8,128)S(1)} %copy-done.9, ...), custom_call_target="tpu_custom_call" | custom-call | flops 60000000 | bytes 60000000 | tf_op jit(solution)/shard_map/pallas_call | solution.py:431
  67.1 0.0 copy-start.1
  67.1 0.9 copy-done.1
  68.0 0.0 all-to-all-done
  68.0 0.1 broadcast_in_dim.13.col_ref
  68.0 1.1 copy-done.2
  69.2 0.7 copy-done.5
  69.9 4.4 %shard_map.96 = (f32[5,9,48,128]{3,2,1,0:T(8,128)S(1)}, f32[48,128]{1,0:T(8,128)S(1)}, f32[4,128]{1,0:T(4,128)S(1)}, f32[4,128]{1,0:T(4,128)S(1)}, f32[8,128]{1,0:T(8,128)S(1)}) custom-call(f32[7,7]{1,0:T(8,128)S(1)} %copy-done.7, f32[4,8,48,128]{3,2,1,0:T(8,128)S(1)} %get-tuple-element.36.x_ref, f32[4,8,48,128]{3,2,1,0:T(8,128)S(1)} %copy-done.2, ...), custom_call_target="tpu_custom_call" | custom-call | flops 4000000 | bytes 4000000 | tf_op jit(solution)/shard_map/pallas_call | solution.py:431
  74.3 0.0 copy-start.6
  74.3 0.1 collective-permute-start.4
  74.5 1.1 collective-permute-done.4
  75.6 0.6 broadcast_in_dim.14
  76.2 19.0 %all-to-all-start.1 = ((f32[32,4,128]{2,1,0:T(4,128)}), f32[32,4,128]{2,1,0:T(4,128)S(1)}, u32[]{:S(2)}, u32[]{:S(2)}) async-start(f32[32,4,128]{2,1,0:T(4,128)} %broadcast_in_dim.14), calls=%async_computation.1 | async-start | bytes 131072 | tf_op jit(solution)/shard_map/all_to_all | solution.py:477
  95.3 8.1 %shard_map.97 = (f32[4,9,40,128]{3,2,1,0:T(8,128)S(1)}, f32[4,9,40,128]{3,2,1,0:T(8,128)S(1)}) custom-call(f32[7,7]{1,0:T(8,128)S(1)} %copy-done.7, f32[5,9,48,128]{3,2,1,0:T(8,128)S(1)} %get-tuple-element.41.dyn_in, f32[8,48,128]{2,1,0:T(8,128)S(1)} %get-tuple-element.42.r_ref, f32[48,128]{1,0:T(8,128)S(1)} %get-tuple-element.43.r8_ref), custom_call_target="tpu_custom_call" | custom-call | flops 50000000 | bytes 50000000 | tf_op jit(solution)/shard_map/pallas_call | solution.py:431
  103.3 0.0 copy-start.3
  103.3 0.9 copy-done.3
  104.2 16.6 %all-to-all-done.1 = f32[32,4,128]{2,1,0:T(4,128)S(1)} async-done(((f32[32,4,128]{2,1,0:T(4,128)}), f32[32,4,128]{2,1,0:T(4,128)S(1)}, u32[]{:S(2)}, u32[]{:S(2)}) %all-to-all-start.1) | async-done | bytes 65568 | tf_op jit(solution)/shard_map/all_to_all | solution.py:477
  120.8 0.0 copy-done.6
  120.8 1.1 copy-done.4
  121.9 3.2 %shard_map.98 = (f32[5,9,40,128]{3,2,1,0:T(8,128)S(1)}, f32[4,128]{1,0:T(4,128)S(1)}, f32[4,128]{1,0:T(4,128)S(1)}, f32[8,128]{1,0:T(8,128)S(1)}) custom-call(f32[7,7]{1,0:T(8,128)S(1)} %copy-done.7, f32[4,9,40,128]{3,2,1,0:T(8,128)S(1)} %get-tuple-element.44.x_ref, f32[4,9,40,128]{3,2,1,0:T(8,128)S(1)} %copy-done.4, ...), custom_call_target="tpu_custom_call" | custom-call | flops 4000000 | bytes 4000000 | tf_op jit(solution)/shard_map/pallas_call | solution.py:431
  125.1 0.1 collective-permute-start.5
  125.2 1.1 collective-permute-done.5
  126.3 0.6 broadcast_in_dim.15
  127.0 5.5 %all-to-all-start.2 = ((f32[32,4,128]{2,1,0:T(4,128)}), f32[32,4,128]{2,1,0:T(4,128)S(1)}, u32[]{:S(2)}, u32[]{:S(2)}) async-start(f32[32,4,128]{2,1,0:T(4,128)} %broadcast_in_dim.15), calls=%async_computation.2 | async-start | bytes 131072 | tf_op jit(solution)/shard_map/all_to_all | solution.py:477
  132.5 6.6 %shard_map.99 = (f32[4,9,32,128]{3,2,1,0:T(8,128)S(1)}, f32[4,9,32,128]{3,2,1,0:T(8,128)S(1)}) custom-call(f32[7,7]{1,0:T(8,128)S(1)} %copy-done.7, f32[5,9,40,128]{3,2,1,0:T(8,128)S(1)} %get-tuple-element.49.dyn_in, f32[8,48,128]{2,1,0:T(8,128)S(1)} %get-tuple-element.42.r_ref, f32[48,128]{1,0:T(8,128)S(1)} %get-tuple-element.43.r8_ref), custom_call_target="tpu_custom_call" | custom-call | flops 40000000 | bytes 40000000 | tf_op jit(solution)/shard_map/pallas_call | solution.py:431
  139.1 18.9 %all-to-all-done.2 = f32[32,4,128]{2,1,0:T(4,128)S(1)} async-done(((f32[32,4,128]{2,1,0:T(4,128)}), f32[32,4,128]{2,1,0:T(4,128)S(1)}, u32[]{:S(2)}, u32[]{:S(2)}) %all-to-all-start.2) | async-done | bytes 65568 | tf_op jit(solution)/shard_map/all_to_all | solution.py:477
  158.0 3.3 %shard_map.100 = (f32[3,32,1080]{2,1,0:T(8,128)}, f32[32,1080]{1,0:T(8,128)}, f32[3]{0:T(128)}) custom-call(f32[7,7]{1,0:T(8,128)S(1)} %copy-done.7, f32[4,9,32,128]{3,2,1,0:T(8,128)S(1)} %get-tuple-element.50.x_ref, f32[4,9,32,128]{3,2,1,0:T(8,128)S(1)} %get-tuple-element.51.y_ref, f32[48,128]{1,0:T(8,128)S(1)} %get-tuple-element.43.r8_ref, ...), custom_call_target="tpu_custom_call" | custom-call | flops 4000000 | bytes 4000000 | tf_op jit(solution)/shard_map/pallas_call | solution.py:431
  (10 shorter events, 0.1 us)
Async XLA Ops:
  0.6 2.5 %copy-start = (s32[1024]{0:T(1024)S(1)}, s32[1024]{0:T(1024)}, u32[]{:S(2)}) copy-start(s32[1024]{0:T(1024)} %param.12) | copy-start | bytes 12292
  2.4 52.5 %copy-start.7 = (f32[7,7]{1,0:T(8,128)S(1)}, f32[7,7]{1,0:T(8,128)}, u32[]{:S(2)}) copy-start(f32[7,7]{1,0:T(8,128)} %w_ref.11) | copy-start | bytes 592
  2.5 1.4 collective-permute-start.1
  2.6 1.5 collective-permute-start
  4.8 0.7 copy-start.8
  5.4 62.5 %all-to-all-start = ((f32[32,4,128]{2,1,0:T(4,128)}), f32[32,4,128]{2,1,0:T(4,128)}, u32[]{:S(2)}, u32[]{:S(2)}) async-start(f32[32,4,128]{2,1,0:T(4,128)} %get-tuple-element.40), calls=%async_computation | async-start | bytes 131072 | tf_op jit(solution)/shard_map/all_to_all | solution.py:461
  38.1 14.5 %collective-permute-start.2 = (f32[9,9,8,128]{3,2,1,0:T(8,128)S(1)}, f32[9,9,8,128]{3,2,1,0:T(8,128)S(1)}, u32[]{:S(2)}, u32[]{:S(2)}) collective-permute-start(f32[9,9,8,128]{3,2,1,0:T(8,128)S(1)} %get-tuple-element.34), channel_id=1, source_target_pairs={{2,0},{4,2},{6,4},{8,6},{10,8},{12,10},{14,12},{16,14},{18,16},{20... | collective-permute-start | bytes 995336 | tf_op jit(solution)/shard_map/ppermute | solution.py:460
  41.0 13.9 %collective-permute-start.3 = (f32[9,9,8,128]{3,2,1,0:T(8,128)S(1)}, f32[9,9,8,128]{3,2,1,0:T(8,128)S(1)}, u32[]{:S(2)}, u32[]{:S(2)}) collective-permute-start(f32[9,9,8,128]{3,2,1,0:T(8,128)S(1)} %get-tuple-element.35), channel_id=1, source_target_pairs={{0,2},{2,4},{4,6},{6,8},{8,10},{10,12},{12,14},{14,16},{16,18},{18... | collective-permute-start | bytes 995336 | tf_op jit(solution)/shard_map/ppermute | solution.py:459
  54.9 0.9 copy-start.9
  67.1 0.9 copy-start.1
  68.0 1.1 copy-start.2
  69.2 0.7 copy-start.5
  74.3 46.5 %copy-start.6 = (bf16[64,96]{1,0:T(8,128)(2,1)S(1)}, bf16[64,96]{1,0:T(8,128)(2,1)}, u32[]{:S(2)}) copy-start(bf16[64,96]{1,0:T(8,128)(2,1)} %add_convert_fusion.sel_ref) | copy-start | bytes 36868
  74.3 1.3 collective-permute-start.4
  76.2 44.5 %all-to-all-start.1 = ((f32[32,4,128]{2,1,0:T(4,128)}), f32[32,4,128]{2,1,0:T(4,128)S(1)}, u32[]{:S(2)}, u32[]{:S(2)}) async-start(f32[32,4,128]{2,1,0:T(4,128)} %broadcast_in_dim.14), calls=%async_computation.1 | async-start | bytes 131072 | tf_op jit(solution)/shard_map/all_to_all | solution.py:477
  103.3 0.9 copy-start.3
  120.8 1.1 copy-start.4
  125.1 1.3 collective-permute-start.5
  127.0 31.0 %all-to-all-start.2 = ((f32[32,4,128]{2,1,0:T(4,128)}), f32[32,4,128]{2,1,0:T(4,128)S(1)}, u32[]{:S(2)}, u32[]{:S(2)}) async-start(f32[32,4,128]{2,1,0:T(4,128)} %broadcast_in_dim.15), calls=%async_computation.2 | async-start | bytes 131072 | tf_op jit(solution)/shard_map/all_to_all | solution.py:477

commit v4 on v3

--- a/solution.py
+++ b/solution.py
@@ -114,7 +114,7 @@
     return d, mc, e, q, over, oc, rc
 
 
-def second_kernel(nrows, f_ref, lat_in, chunk_ref, sum_ref, sum_in, t8_ref, low_ref, high_ref, send_ref):
+def second_kernel(nrows, f_in, lat_in, chunk_ref, sum_ref, sum_in, f_ref, low_ref, high_ref, send_ref):
     nt = f_ref.shape[1]
     ncols = f_ref.shape[2]
     edge = nrows - (nt - 1) * LANES
@@ -124,14 +124,13 @@
     keep = jnp.where(north, (lane >= LANES - HALO).astype(jnp.int32), ((lane >= edge) & (lane < edge + HALO)).astype(jnp.int32)) > 0
     for f in range(8):
         got = jnp.where(north, pltpu.roll(lat_in[f], (LANES - edge) % LANES, 1), pltpu.roll(lat_in[f], edge, 1))
-        t8_ref[f] = jnp.where(own, f_ref[f, nt - 1], jnp.where(keep, got, 0.0))
+        f_ref[f, nt - 1] = jnp.where(own, f_ref[f, nt - 1], jnp.where(keep, got, 0.0))
     for f in range(8):
         for c in range(nt):
-            at = t8_ref.at[f] if c == nt - 1 else f_ref.at[f, c]
-            low_ref[f, c] = at[0:8]
-            low_ref[8, c, f : f + 1] = at[8:9]
-            high_ref[f, c] = at[ncols - 8 : ncols]
-            high_ref[8, c, f : f + 1] = at[ncols - 9 : ncols - 8]
+            low_ref[f, c] = f_ref[f, c, 0:8]
+            low_ref[8, c, f : f + 1] = f_ref[f, c, 8:9]
+            high_ref[f, c] = f_ref[f, c, ncols - 8 : ncols]
+            high_ref[8, c, f : f + 1] = f_ref[f, c, ncols - 9 : ncols - 8]
     s = sum_ref[0:1, :] + sum_in[0:1, :]
     chunk = [chunk_ref[k : k + 1, :] for k in range(4)]
     chunk[3] = chunk[3] + s
@@ -140,7 +139,7 @@
         send_ref[n] = block
 
 
-def ghosts(got_ref, sel_ref, col_ref):
+def ghosts(got_ref, partner_ref):
     n = got_ref.shape[0] // 4
     parts = []
     for r in range(4):
@@ -150,9 +149,14 @@
         h2 = m.astype(jnp.bfloat16)
         h3 = (m - h2.astype(F32)).astype(jnp.bfloat16)
         parts.append(jnp.concatenate([h, h2, h3], axis=0))
-    picked = jnp.dot(sel_ref[...], jnp.concatenate(parts, axis=1), preferred_element_type=F32)
-    lane = lax.broadcasted_iota(jnp.int32, (sel_ref.shape[0], LANES), 1)
-    col = col_ref[...] == (lane & 31)
+    partner = partner_ref[...]
+    rows = partner.shape[0]
+    source, place = partner >> 5, partner & 31
+    one_hot = source[:, 0 : 3 * n] == (lax.broadcasted_iota(jnp.int32, (rows, 3 * n), 1) % n)
+    sel = jnp.where(one_hot, 1.0, 0.0).astype(jnp.bfloat16)
+    picked = jnp.dot(sel, jnp.concatenate(parts, axis=1), preferred_element_type=F32)
+    lane = lax.broadcasted_iota(jnp.int32, (rows, LANES), 1)
+    col = place == (lane & 31)
     group = lane >> 5
     picked = [jnp.where(col, picked[:, r * LANES : (r + 1) * LANES], 0.0) for r in range(4)]
     out = []
@@ -206,8 +210,19 @@
     return jnp.sum(got_ref[pl.ds(3, got_ref.shape[0] // 4, stride=4), :], axis=0, keepdims=True)
 
 
-def ghost_sums(w_ref, got_ref, sel_ref, col_ref, gg_ref, ga_ref, factor, edge, first, start, tiles):
-    gh = ghosts(got_ref, sel_ref, col_ref)
+def edge_weights(w_ref, wl_ref, edge):
+    lane = lax.broadcasted_iota(jnp.int32, (1, LANES), 1)
+    at = jnp.where(is_north(), edge - 1, -4)
+    for k in range(3):
+        for a in range(7):
+            t = jnp.zeros((1, LANES), F32)
+            for m in range(3 - k):
+                t = jnp.where(lane == at - m, w_ref[a, 4 + k + m], t)
+            wl_ref[7 * k + a : 7 * k + a + 1, :] = t
+
+
+def ghost_sums(wl_ref, got_ref, partner_ref, gg_ref, factor, first, start, tiles):
+    gh = ghosts(got_ref, partner_ref)
     d, q = gh[0], gh[1]
     if first:
         oc = [jnp.where(v > 0.0, 1.0, 0.0) for v in q]
@@ -218,15 +233,24 @@
         vals.append([gh[2 + m][k] * (1.0 - factor * q[k]) for k in range(3)])
     if first:
         vals.append(oc)
-    shape = gg_ref.shape[2:]
-    lane = lax.broadcasted_iota(jnp.int32, shape, 1)
-    at = jnp.where(is_north(), edge, -4)
     for f, v in enumerate(vals):
-        t = jnp.zeros(shape, F32)
         for k in range(3):
-            t = jnp.where(lane == at + k, v[k], t)
-        gg_ref[f, 0] = t
-    smooth_into(w_ref, gg_ref, ga_ref, len(vals), start, tiles)
+            gg_ref[3 * f + k] = jnp.broadcast_to(v[k], gg_ref.shape[1:])
+    wl = [wl_ref[n : n + 1, :] for n in range(21)]
+    out = []
+    for f in range(len(vals)):
+        sums = []
+        for i in range(tiles):
+            row = start + 8 * i
+            t = None
+            for k in range(3):
+                u = gg_ref[3 * f + k, row - 3 : row + 5, :] * wl[7 * k]
+                for a in range(1, 7):
+                    u = u + gg_ref[3 * f + k, row + a - 3 : row + a + 5, :] * wl[7 * k + a]
+                t = u if t is None else t + u
+            sums.append(t)
+        out.append(sums)
+    return out
 
 
 def coefficients(r, g, acc):
@@ -243,10 +267,17 @@
         g_ref[5 + k, c, at, :] = e[k] * q
 
 
-def ahead_first(w_ref, f_ref, t8_ref, low_in, high_in, x_ref, y_ref, stat_ref, r_ref, edge_ref, g_ref, acc_ref):
+def ahead_first(
+    edge, w_ref, f_ref, low_hbm, high_hbm, y_hbm, stat_ref, r_ref, edge_ref, wl_ref,
+    g_ref, acc_ref, low_in, high_in, y_ref, sem, y_sem,
+):
+    copies = [pltpu.make_async_copy(high_hbm, high_in, sem.at[0]), pltpu.make_async_copy(low_hbm, low_in, sem.at[1])]
+    for copy in copies:
+        copy.start()
     nt = f_ref.shape[1]
     ncols = f_ref.shape[2]
-    n = x_ref.shape[2]
+    n = stat_ref.shape[2]
+    edge_weights(w_ref, wl_ref, edge)
 
     def local(vals, c, row, nr):
         d, _, e, q, _, oc, rc = start_state(vals)
@@ -260,11 +291,13 @@
             stat_ref[3, c, to, :] = rc
 
     for c in range(nt):
+        for i in range(ncols // 8):
+            local([f_ref[f, c, 8 * i : 8 * i + 8, :] for f in range(8)], c, PAD + 8 * i, 8)
+    for copy in copies:
+        copy.wait()
+    for c in range(nt):
         local([high_in[8, c, f : f + 1, :] for f in range(8)], c, PAD - 9, 1)
         local([high_in[f, c] for f in range(8)], c, PAD - 8, 8)
-        for i in range(ncols // 8):
-            at = slice(8 * i, 8 * i + 8)
-            local([(t8_ref[f, at, :] if c == nt - 1 else f_ref[f, c, at, :]) for f in range(8)], c, PAD + 8 * i, 8)
         local([low_in[f, c] for f in range(8)], c, PAD + ncols, 8)
         local([low_in[8, c, f : f + 1, :] for f in range(8)], c, PAD + ncols + 8, 1)
     smooth_into(w_ref, g_ref, acc_ref, 9, 8, n // 8)
@@ -275,16 +308,19 @@
             r_ref[c, to, :] = r
             x, y = coefficients(r, [g_ref[f, c, at, :] for f in range(8)], [acc_ref[f, c, to, :] for f in range(8)])
             for f in range(4):
-                x_ref[f, c, to, :] = x[f]
-                y_ref[f, c, to, :] = y[f]
+                y_ref[i, f, c] = x[f]
+                y_ref[i, 4 + f, c] = y[f]
+        pltpu.make_async_copy(y_ref.at[i], y_hbm.at[i], y_sem.at[i]).start()
         for f in range(9):
             edge_ref[f, to, :] = g_ref[f, nt - 1, at, :]
             edge_ref[9 + f, to, :] = acc_ref[f, nt - 1, to, :]
-
-
-def ahead_later(skip, w_ref, dyn_in, r_ref, r8_ref, x_ref, y_ref, g_ref, acc_ref):
+    for i in range(n // 8):
+        pltpu.make_async_copy(y_ref.at[i], y_hbm.at[i], y_sem.at[i]).wait()
+
+
+def ahead_later(skip, w_ref, dyn_in, r_ref, r8_ref, y_hbm, g_ref, acc_ref, y_ref, y_sem):
     nt = dyn_in.shape[1]
-    n = x_ref.shape[2]
+    n = 8 * y_ref.shape[0]
     for i in range(dyn_in.shape[2] // 8):
         at = slice(8 * i, 8 * i + 8)
         for c in range(nt):
@@ -296,8 +332,11 @@
             r = r8_ref[fr, :] if c == nt - 1 else r_ref[c, fr, :]
             x, y = coefficients(r, [g_ref[f, c, at, :] for f in range(8)], [acc_ref[f, c, to, :] for f in range(8)])
             for f in range(4):
-                x_ref[f, c, to, :] = x[f]
-                y_ref[f, c, to, :] = y[f]
+                y_ref[i, f, c] = x[f]
+                y_ref[i, 4 + f, c] = y[f]
+        pltpu.make_async_copy(y_ref.at[i], y_hbm.at[i], y_sem.at[i]).start()
+    for i in range(n // 8):
+        pltpu.make_async_copy(y_ref.at[i], y_hbm.at[i], y_sem.at[i]).wait()
 
 
 def next_state(c, at, to, new, stat_ref, dyn_ref):
@@ -325,12 +364,14 @@
 
 
 def after_first(
-    nrows, ncols, w_ref, x_ref, y_ref, stat_ref, edge_ref, got_ref, sel_ref, col_ref,
-    dyn_ref, r8_ref, chunk_ref, sum_ref, mean_ref, gg_ref, ga_ref,
+    edge, ncols, wl_ref, y_hbm, stat_ref, edge_ref, got_ref, partner_ref,
+    dyn_ref, r8_ref, chunk_ref, sum_ref, mean_ref, gg_ref, y_ref, sem,
 ):
-    nt = x_ref.shape[1] + 1
-    n = x_ref.shape[2]
-    edge = nrows - (nt - 1) * LANES
+    copies = [pltpu.make_async_copy(y_hbm.at[i], y_ref.at[i], sem.at[i]) for i in range(y_ref.shape[0])]
+    for copy in copies:
+        copy.start()
+    nt = y_ref.shape[2] + 1
+    n = 8 * y_ref.shape[0]
     sums = received_sums(got_ref)
     count = lane_value(sums, 97) + 1.0
     mean = lane_value(sums, 96) / count
@@ -339,19 +380,20 @@
     mean_ref[...] = jnp.where(lane1 == 1, mean, count)
     lane = lax.broadcasted_iota(jnp.int32, (8, LANES), 1)
     f8 = jnp.broadcast_to(factor, (8, LANES))
-    ghost_sums(w_ref, got_ref, sel_ref, col_ref, gg_ref, ga_ref, factor, edge, True, 8, n // 8)
+    ga = ghost_sums(wl_ref, got_ref, partner_ref, gg_ref, factor, True, 8, n // 8)
     excess = jnp.zeros((8, LANES), F32)
     for i in range(n // 8):
+        copies[i].wait()
         at = slice(8 * i, 8 * i + 8)
         own = PAD - 8 <= 8 * i < PAD - 8 + ncols
         for c in range(nt):
             if c == nt - 1:
-                r = 0.5 * edge_ref[8, at, :] / (edge_ref[17, at, :] + ga_ref[4, 0, at, :] + 1.0)
+                r = 0.5 * edge_ref[8, at, :] / (edge_ref[17, at, :] + ga[4][i] + 1.0)
                 r8_ref[at, :] = r
                 x, y = coefficients(r, [edge_ref[f, at, :] for f in range(8)], [edge_ref[9 + f, at, :] for f in range(8)])
-                new = [x[f] + f8 * y[f] + r * ga_ref[f, 0, at, :] for f in range(4)]
+                new = [x[f] + f8 * y[f] + r * ga[f][i] for f in range(4)]
             else:
-                new = [x_ref[f, c, at, :] + f8 * y_ref[f, c, at, :] for f in range(4)]
+                new = [y_ref[i, f, c] + f8 * y_ref[i, 4 + f, c] for f in range(4)]
             over = next_state(c, at, at, new, stat_ref, dyn_ref)
             if own:
                 excess = excess + (jnp.where(lane < edge, over, 0.0) if c == nt - 1 else over)
@@ -359,12 +401,14 @@
 
 
 def after_second(
-    nrows, ncols, w_ref, x_ref, y_ref, stat_ref, r8_ref, got_ref, sel_ref, col_ref, mean_in,
-    dyn_ref, chunk_ref, sum_ref, mean_ref, gg_ref, ga_ref,
+    edge, ncols, wl_ref, y_hbm, stat_ref, r8_ref, got_ref, partner_ref, mean_in,
+    dyn_ref, chunk_ref, sum_ref, mean_ref, gg_ref, y_ref, sem,
 ):
-    nt = x_ref.shape[1]
-    n = x_ref.shape[2]
-    edge = nrows - (nt - 1) * LANES
+    copies = [pltpu.make_async_copy(y_hbm.at[i], y_ref.at[i], sem.at[i]) for i in range(y_ref.shape[0])]
+    for copy in copies:
+        copy.start()
+    nt = y_ref.shape[2]
+    n = 8 * y_ref.shape[0]
     mean = lane_value(received_sums(got_ref), 96) / lane_value(mean_in[0:1, :], 0)
     factor = 1.0 / (1.0 + 2.0 * mean)
     lane1 = lax.broadcasted_iota(jnp.int32, mean_ref.shape, 1)
@@ -372,14 +416,15 @@
     lane = lax.broadcasted_iota(jnp.int32, (8, LANES), 1)
     row = lax.broadcasted_iota(jnp.int32, (8, LANES), 0)
     f8 = jnp.broadcast_to(factor, (8, LANES))
-    ghost_sums(w_ref, got_ref, sel_ref, col_ref, gg_ref, ga_ref, factor, edge, False, 12, n // 8)
+    ga = ghost_sums(wl_ref, got_ref, partner_ref, gg_ref, factor, False, 12, n // 8)
     excess = jnp.zeros((8, LANES), F32)
     for i in range(n // 8):
+        copies[i].wait()
         at, to = slice(4 + 8 * i, 12 + 8 * i), slice(8 * i, 8 * i + 8)
         for c in range(nt):
-            new = [x_ref[f, c, to, :] + f8 * y_ref[f, c, to, :] for f in range(4)]
+            new = [y_ref[i, f, c] + f8 * y_ref[i, 4 + f, c] for f in range(4)]
             if c == nt - 1:
-                new = [new[f] + r8_ref[at, :] * ga_ref[f, 0, to, :] for f in range(4)]
+                new = [new[f] + r8_ref[at, :] * ga[f][i] for f in range(4)]
             over = next_state(c, at, to, new, stat_ref, dyn_ref)
             if 8 * i < 4:
                 over = jnp.where(row >= 4, over, 0.0)
@@ -390,69 +435,79 @@
 
 
 def after_third(
-    nrows, ncols, w_ref, x_ref, y_ref, r8_ref, got_ref, sel_ref, col_ref, mean_in,
-    stress_ref, damage_ref, mean_ref, gg_ref, ga_ref,
+    nrows, wl_ref, y_hbm, r8_ref, got_ref, partner_ref, mean_in,
+    stress_hbm, damage_hbm, mean_ref, gg_ref, y_ref, out_ref, sem, out_sem,
 ):
-    nt = x_ref.shape[1]
-    edge = nrows - (nt - 1) * LANES
+    copies = [pltpu.make_async_copy(y_hbm.at[i], y_ref.at[i], sem.at[i]) for i in range(y_ref.shape[0])]
+    for copy in copies:
+        copy.start()
+    nt = y_ref.shape[2]
+    ncols = 8 * y_ref.shape[0]
     row = mean_in[0:1, :]
     mean = lane_value(received_sums(got_ref), 96) / lane_value(row, 0)
     factor = 1.0 / (1.0 + 2.0 * mean)
     for at, one in enumerate((lane_value(row, 1), lane_value(row, 2), mean)):
         mean_ref[at] = jnp.sum(one)
     f8 = jnp.broadcast_to(factor, (8, LANES))
-    ghost_sums(w_ref, got_ref, sel_ref, col_ref, gg_ref, ga_ref, factor, edge, False, PAD, ncols // 8)
-    for c in range(nt):
-        w = min(LANES, nrows - c * LANES)
-        for i in range(ncols // 8):
-            at = slice(8 * i, 8 * i + 8)
-            for f in range(4):
-                v = x_ref[f, c, at, :] + f8 * y_ref[f, c, at, :]
+    ga = ghost_sums(wl_ref, got_ref, partner_ref, gg_ref, factor, False, PAD, ncols // 8)
+    outs = []
+    for i in range(ncols // 8):
+        copies[i].wait()
+        at = slice(8 * i, 8 * i + 8)
+        for f in range(4):
+            for c in range(nt):
+                w = min(LANES, nrows - c * LANES)
+                v = y_ref[i, f, c] + f8 * y_ref[i, 4 + f, c]
                 if c == nt - 1:
-                    v = v + r8_ref[8 + 8 * i : 16 + 8 * i, :] * ga_ref[f, 0, at, :]
-                if f == 0:
-                    damage_ref[at, c * LANES : c * LANES + w] = v[:, 0:w]
-                else:
-                    stress_ref[f - 1, at, c * LANES : c * LANES + w] = v[:, 0:w]
+                    v = v + r8_ref[8 + 8 * i : 16 + 8 * i, :] * ga[f][i]
+                out_ref[f, at, c * LANES : c * LANES + w] = v[:, 0:w]
+            to = damage_hbm.at[pl.ds(8 * i, 8)] if f == 0 else stress_hbm.at[f - 1, pl.ds(8 * i, 8)]
+            outs.append(pltpu.make_async_copy(out_ref.at[f, pl.ds(8 * i, 8)], to, out_sem.at[4 * i + f]))
+            outs[-1].start()
+    for one in outs:
+        one.wait()
 
 
 def step(strain_rate, stress_start, concentration, cell_class, land_mask, fold_partner, kernel_weights):
     ncols, nrows = concentration.shape
     nt = -(-nrows // LANES)
+    edge = nrows - (nt - 1) * LANES
     nlon = lax.axis_size("lon")
     nlat = lax.axis_size("lat")
     rows = ncols + 2 * PAD
     n1, n2 = rows - 16, rows - 24
     sds = lambda *s: jax.ShapeDtypeStruct(s, F32)
     vmem = lambda *s: pltpu.VMEM(s, F32)
-
-    def call(body, flops, *args, weights=True, **kw):
-        given = args if not weights else (kernel_weights, *args)
+    dma = lambda n: pltpu.SemaphoreType.DMA((n,))
+    far = lambda a: pltpu.with_memory_space_constraint(a, pltpu.HBM)
+    hbm = pl.BlockSpec(memory_space=pltpu.HBM)
+    anywhere = pl.BlockSpec(memory_space=pl.ANY)
+    hds = lambda *s: pltpu.HBM(s, F32)
+
+    def call(body, flops, args, out_shape, scratch=(), weights=False, in_far=(), in_any=(), out_far=(), scalars=(), **kw):
+        specs = [hbm if n in in_far else anywhere if n in in_any else VM for n in range(len(args))]
+        args = [far(a) if n in in_far else a for n, a in enumerate(args)]
         return pl.pallas_call(
-            body, in_specs=([SM] if weights else []) + [VM] * len(args), cost_estimate=cost(flops, flops),
-            compiler_params=small(), **kw,
-        )(*given)
+            body, in_specs=[SM] * weights + specs, out_shape=out_shape, scratch_shapes=scratch,
+            out_specs=tuple(hbm if n in out_far else SM if n in scalars else VM for n in range(len(out_shape))),
+            cost_estimate=cost(flops, flops), compiler_params=small(), **kw,
+        )(*[kernel_weights] * weights, *args)
 
     columns = (lax.axis_index("lon") * ncols - PAD + jnp.arange(rows, dtype=jnp.int32)) % (ncols * nlon)
-    partner = jnp.take(fold_partner, columns)
-    sel = (partner[:, None] // ncols == jnp.arange(nlon)[None, :]).astype(jnp.bfloat16)
-    sel = jnp.concatenate([sel, sel, sel], axis=1)
-    col = jnp.broadcast_to((partner % ncols)[:, None], (rows, LANES)).astype(jnp.int32)
+    partner = jnp.broadcast_to(jnp.take(fold_partner, columns)[:, None], (rows, LANES))
 
     given = (strain_rate, stress_start, concentration, cell_class, land_mask)
-    f, lat_out, chunk, sums = pl.pallas_call(
-        functools.partial(first_kernel, nrows),
-        out_shape=(sds(8, nt, ncols, LANES), sds(8, ncols, LANES), sds(4, LANES), sds(8, LANES)),
-        in_specs=[pl.BlockSpec(memory_space=pltpu.HBM)] * 5, out_specs=(VM,) * 4,
-        scratch_shapes=[pltpu.VMEM(a.shape, a.dtype) for a in given] + [pltpu.SemaphoreType.DMA((5,))],
-        cost_estimate=cost(4000000, 2000000), compiler_params=small(), name="first",
-    )(*(pltpu.with_memory_space_constraint(a, pltpu.HBM) for a in given))
+    f, lat_out, chunk, sums = call(
+        functools.partial(first_kernel, nrows), 4000000, given,
+        (sds(8, nt, ncols, LANES), sds(8, ncols, LANES), sds(4, LANES), sds(8, LANES)),
+        [pltpu.VMEM(a.shape, a.dtype) for a in given] + [dma(5)], in_far=range(5),
+    )
     swap = [(i, nlat - 1 - i) for i in range(nlat)]
     lat_in = lax.ppermute(lat_out, "lat", swap)
     sum_in = lax.ppermute(sums, "lat", swap)
-    t8, low, high, send = call(
-        functools.partial(second_kernel, nrows), 400000, f, lat_in, chunk, sums, sum_in, weights=False,
-        out_shape=(sds(8, ncols, LANES), sds(9, nt, 8, LANES), sds(9, nt, 8, LANES), sds(nlon, 4, LANES)), out_specs=(VM,) * 4,
+    f, low, high, send = call(
+        functools.partial(second_kernel, nrows), 400000, (f, lat_in, chunk, sums, sum_in),
+        (sds(8, nt, ncols, LANES), sds(9, nt, 8, LANES), sds(9, nt, 8, LANES), sds(nlon, 4, LANES)), input_output_aliases={0: 0},
     )
     up = [(i, (i + 1) % nlon) for i in range(nlon)]
     down = [(j, i) for i, j in up]
@@ -460,15 +515,18 @@
     low_in = lax.ppermute(low, "lon", down)
     got = lax.all_to_all(send, "lon", 0, 0, tiled=True).reshape(nlon * 4, LANES)
 
-    x, y, stat, r, edge = call(
-        ahead_first, 60000000, f, t8, low_in, high_in,
-        out_shape=(sds(4, nt - 1, n1, LANES), sds(4, nt - 1, n1, LANES), sds(4, nt, n1, LANES), sds(nt - 1, n1, LANES), sds(18, n1, LANES)),
-        out_specs=(VM,) * 5, scratch_shapes=[vmem(9, nt, rows, LANES), vmem(9, nt, n1, LANES)],
+    strip = vmem(9, nt, 8, LANES)
+    y1, y2, y3 = (n1 // 8, 8, nt - 1, 8, LANES), (n2 // 8, 8, nt, 8, LANES), (ncols // 8, 8, nt, 8, LANES)
+    y, stat, r, raw, wl = call(
+        functools.partial(ahead_first, edge), 60000000, (f, low_in, high_in),
+        (hds(*y1), sds(4, nt, n1, LANES), sds(nt - 1, n1, LANES), sds(18, n1, LANES), sds(24, LANES)),
+        [vmem(9, nt, rows, LANES), vmem(9, nt, n1, LANES), strip, strip, vmem(*y1), dma(2), dma(n1 // 8)],
+        weights=True, in_any=(1, 2), out_far=(0,),
     )
     dyn, r8, chunk, sums, mean = call(
-        functools.partial(after_first, nrows, ncols), 4000000, x, y, stat, edge, got, sel, col,
-        out_shape=(sds(5, nt, n1, LANES), sds(n1, LANES), sds(4, LANES), sds(4, LANES), sds(8, LANES)),
-        out_specs=(VM,) * 5, scratch_shapes=[vmem(5, 1, rows, LANES), vmem(5, 1, n1, LANES)],
+        functools.partial(after_first, edge, ncols), 4000000, (wl, y, stat, raw, got, partner),
+        (sds(5, nt, n1, LANES), sds(n1, LANES), sds(4, LANES), sds(4, LANES), sds(8, LANES)),
+        [vmem(15, rows, LANES), vmem(*y1), dma(n1 // 8)], in_far=(1,),
     )
 
     def spread(chunk, sums):
@@ -477,26 +535,23 @@
         return lax.all_to_all(send, "lon", 0, 0, tiled=True).reshape(nlon * 4, LANES)
 
     got = spread(chunk, sums)
-    x, y = call(
-        functools.partial(ahead_later, 4), 50000000, dyn, r, r8,
-        out_shape=(sds(4, nt, n2, LANES), sds(4, nt, n2, LANES)), out_specs=(VM,) * 2,
-        scratch_shapes=[vmem(8, nt, n1, LANES), vmem(8, nt, n2, LANES)],
+    (y,) = call(
+        functools.partial(ahead_later, 4), 50000000, (dyn, r, r8), (hds(*y2),),
+        [vmem(8, nt, n1, LANES), vmem(8, nt, n2, LANES), vmem(*y2), dma(n2 // 8)], weights=True, out_far=(0,),
     )
     dyn, chunk, sums, mean = call(
-        functools.partial(after_second, nrows, ncols), 4000000, x, y, stat, r8, got, sel, col, mean,
-        out_shape=(sds(5, nt, n2, LANES), sds(4, LANES), sds(4, LANES), sds(8, LANES)),
-        out_specs=(VM,) * 4, scratch_shapes=[vmem(4, 1, rows, LANES), vmem(4, 1, n2, LANES)],
+        functools.partial(after_second, edge, ncols), 4000000, (wl, y, stat, r8, got, partner, mean),
+        (sds(5, nt, n2, LANES), sds(4, LANES), sds(4, LANES), sds(8, LANES)), [vmem(12, rows, LANES), vmem(*y2), dma(n2 // 8)], in_far=(1,),
     )
     got = spread(chunk, sums)
-    x, y = call(
-        functools.partial(ahead_later, 8), 40000000, dyn, r, r8,
-        out_shape=(sds(4, nt, ncols, LANES), sds(4, nt, ncols, LANES)), out_specs=(VM,) * 2,
-        scratch_shapes=[vmem(8, nt, n2, LANES), vmem(8, nt, ncols, LANES)],
+    (y,) = call(
+        functools.partial(ahead_later, 8), 40000000, (dyn, r, r8), (hds(*y3),),
+        [vmem(8, nt, n2, LANES), vmem(8, nt, ncols, LANES), vmem(*y3), dma(ncols // 8)], weights=True, out_far=(0,),
     )
     return call(
-        functools.partial(after_third, nrows, ncols), 4000000, x, y, r8, got, sel, col, mean,
-        out_shape=(sds(3, ncols, nrows), sds(ncols, nrows), sds(ITERS)), out_specs=(VM, VM, SM),
-        scratch_shapes=[vmem(4, 1, rows, LANES), vmem(4, 1, ncols, LANES)],
+        functools.partial(after_third, nrows), 4000000, (wl, y, r8, got, partner, mean),
+        (hds(3, ncols, nrows), hds(ncols, nrows), sds(ITERS)),
+        [vmem(12, rows, LANES), vmem(*y3), vmem(4, ncols, nrows), dma(ncols // 8), dma(ncols // 2)], in_far=(1,), out_far=(0, 1), scalars=(2,),
     )
 
 

time: 162 us -> 153 us (0.944)
  local copies, waits for them, and re-layouts: 8.38 us -> 2.1 us
  Pallas kernels: 39.2 us -> 37.5 us
    unnamed x20 -> x4, local copies, waits for them, and re-layouts: 6.29 us -> 0.02 us
    pallas_call x8, Pallas kernels: 39.2 us -> 37.5 us  [call(): pl.pallas_call(body, in_specs=[SM] * weights + specs, out_shape=out_shape...]
  transfers between devices with their start and end apart: 9 -> 9, of which waited for: 7 -> 7; matrix products, arithmetic and copies ran while one was open for 1% -> 1% of each run, Pallas kernels for 16% -> 19%
where the time goes in v4:
time: 153 us; the launch traced here: 152 us
  starting transfers between devices  61.1 us (40%)
  waiting for transfers between devices  50.6 us (33%)
  Pallas kernels  37.5 us (25%)
  local copies, waits for them, and re-layouts  2.1 us (1%)
    pallas_call x8, Pallas kernels, call(): pl.pallas_call(body, in_specs=[SM] * weights + specs, out_shape=out_shape...  37.5 us
    all_to_all x2, waiting for transfers between devices, spread(): lax.all_to_all(send, 'lon', 0, 0, tiled=True).reshape(nlon * 4, LANES)  34.3 us
    all_to_all x1, starting transfers between devices, step(): got = lax.all_to_all(send, 'lon', 0, 0, tiled=True).reshape(nlon * 4, LANES)  32.7 us
    all_to_all x2, starting transfers between devices, spread(): lax.all_to_all(send, 'lon', 0, 0, tiled=True).reshape(nlon * 4, LANES)  24.7 us
    ppermute x1, waiting for transfers between devices, step(): low_in = lax.ppermute(low, 'lon', down)  10.8 us
  transfers between devices with their start and end apart: 9, of which 7 were waited for; matrix products, arithmetic and copies ran while one was open for 1% of the time, Pallas kernels for 19%

profile of v4, /device:TPU:38, one launch (start us, length us, event | category | flops | bytes accessed | tf_op | source)
XLA Modules:
  0.0 152.2 jit_solution(12759166510059981848)
XLA Ops:
  0.6 0.0 copy-start
  0.6 1.8 %shard_map.94 = (f32[8,9,32,128]{3,2,1,0:T(8,128)S(1)}, f32[8,32,128]{2,1,0:T(8,128)S(1)}, f32[4,128]{1,0:T(4,128)S(1)}, f32[8,128]{1,0:T(8,128)S(1)}) custom-call(f32[3,32,1080]{2,1,0:T(8,128)} %refs_0_.1, f32[3,32,1080]{2,1,0:T(8,128)} %refs_1_.1, f32[32,1080]{1,0:T(8,128)} %refs_2_.1, s32[32,1080]{1,0:T(8,128)} %refs_3_.1, s32[32,1080]{1,0:T(8,128)} %refs_4_.1), custom_call_target="tpu_custom_call" | custom-call | flops 4000000 | bytes 4000000 | tf_op jit(solution)/shard_map/pallas_call | solution.py:490
  2.4 0.0 copy-start.1
  2.5 0.1 collective-permute-start
  2.6 0.5 collective-permute-start.1
  3.1 0.8 collective-permute-done.1.sum_in
  3.9 0.0 collective-permute-done.lat_in
  3.9 0.7 shard_map.95
  4.6 32.7 %all-to-all-start = ((f32[32,4,128]{2,1,0:T(4,128)}), f32[32,4,128]{2,1,0:T(4,128)S(1)}, u32[]{:S(2)}, u32[]{:S(2)}) async-start(f32[32,4,128]{2,1,0:T(4,128)} %get-tuple-element.36), calls=%async_computation | async-start | bytes 131072 | tf_op jit(solution)/shard_map/all_to_all | solution.py:516
  37.3 2.9 %collective-permute-start.2 = (f32[9,9,8,128]{3,2,1,0:T(8,128)S(1)}, f32[9,9,8,128]{3,2,1,0:T(8,128)S(1)}, u32[]{:S(2)}, u32[]{:S(2)}) collective-permute-start(f32[9,9,8,128]{3,2,1,0:T(8,128)S(1)} %get-tuple-element.30), channel_id=1, source_target_pairs={{2,0},{4,2},{6,4},{8,6},{10,8},{12,10},{14,12},{16,14},{18,16},{20... | collective-permute-start | bytes 995336 | tf_op jit(solution)/shard_map/ppermute | solution.py:515
  40.2 0.0 collective-permute-start.3
  40.2 0.0 copy-done
  40.2 0.7 gather_fusion
  41.0 10.8 %collective-permute-done.2.low_hbm = f32[9,9,8,128]{3,2,1,0:T(8,128)S(1)} collective-permute-done((f32[9,9,8,128]{3,2,1,0:T(8,128)S(1)}, f32[9,9,8,128]{3,2,1,0:T(8,128)S(1)}, u32[]{:S(2)}, u32[]{:S(2)}) %collective-permute-start.2) | collective-permute-done | bytes 331808 | tf_op jit(solution)/shard_map/ppermute | solution.py:515
  51.8 2.3 %collective-permute-done.3.high_hbm = f32[9,9,8,128]{3,2,1,0:T(8,128)S(1)} collective-permute-done((f32[9,9,8,128]{3,2,1,0:T(8,128)S(1)}, f32[9,9,8,128]{3,2,1,0:T(8,128)S(1)}, u32[]{:S(2)}, u32[]{:S(2)}) %collective-permute-start.3) | collective-permute-done | bytes 331808 | tf_op jit(solution)/shard_map/ppermute | solution.py:514
  54.1 0.0 copy-done.1
  54.1 12.4 %shard_map.96 = (f32[6,8,8,8,128]{4,3,2,1,0:T(8,128)}, f32[4,9,48,128]{3,2,1,0:T(8,128)S(1)}, f32[8,48,128]{2,1,0:T(8,128)S(1)}, f32[18,48,128]{2,1,0:T(8,128)S(1)}, f32[24,128]{1,0:T(8,128)S(1)}) custom-call(f32[7,7]{1,0:T(8,128)S(1)} %copy-done.1, f32[8,9,32,128]{3,2,1,0:T(8,128)S(1)} %get-tuple-element.29.f_ref, ...), custom_call_target="tpu_custom_call" | custom-call | flops 60000000 | bytes 60000000 | tf_op jit(solution)/shard_map/pallas_call | solution.py:490
  66.5 0.0 all-to-all-done
  66.5 0.1 broadcast_in_dim.13.partner_ref
  66.6 1.6 %shard_map.97 = (f32[5,9,48,128]{3,2,1,0:T(8,128)S(1)}, f32[48,128]{1,0:T(8,128)S(1)}, f32[4,128]{1,0:T(4,128)S(1)}, f32[4,128]{1,0:T(4,128)S(1)}, f32[8,128]{1,0:T(8,128)S(1)}) custom-call(f32[24,128]{1,0:T(8,128)S(1)} %get-tuple-element.32.wl_ref, f32[6,8,8,8,128]{4,3,2,1,0:T(8,128)} %get-tuple-element.33.y_hbm, ...), custom_call_target="tpu_custom_call" | custom-call | flops 4000000 | bytes 4000000 | tf_op jit(solution)/shard_map/pallas_call | solution.py:490
  68.3 0.1 collective-permute-start.4
  68.4 1.1 collective-permute-done.4
  69.6 0.6 broadcast_in_dim.14
  70.2 19.0 %all-to-all-start.1 = ((f32[32,4,128]{2,1,0:T(4,128)}), f32[32,4,128]{2,1,0:T(4,128)S(1)}, u32[]{:S(2)}, u32[]{:S(2)}) async-start(f32[32,4,128]{2,1,0:T(4,128)} %broadcast_in_dim.14), calls=%async_computation.1 | async-start | bytes 131072 | tf_op jit(solution)/shard_map/all_to_all | solution.py:535
  89.2 9.1 %shard_map.98.y_hbm = f32[5,8,9,8,128]{4,3,2,1,0:T(8,128)} custom-call(f32[7,7]{1,0:T(8,128)S(1)} %copy-done.1, f32[5,9,48,128]{3,2,1,0:T(8,128)S(1)} %get-tuple-element.37.dyn_in, f32[8,48,128]{2,1,0:T(8,128)S(1)} %get-tuple-element.38.r_ref, f32[48,128]{1,0:T(8,128)S(1)} %get-tuple-element.39.r8_ref), custom_call_target="tpu_custom_call" | custom-call | flops 50000000 | bytes 50000000 | tf_op jit(solution)/shard_map/pallas_call | solution.py:490
  98.3 16.4 %all-to-all-done.1 = f32[32,4,128]{2,1,0:T(4,128)S(1)} async-done(((f32[32,4,128]{2,1,0:T(4,128)}), f32[32,4,128]{2,1,0:T(4,128)S(1)}, u32[]{:S(2)}, u32[]{:S(2)}) %all-to-all-start.1) | async-done | bytes 65568 | tf_op jit(solution)/shard_map/all_to_all | solution.py:535
  114.7 1.6 %shard_map.99 = (f32[5,9,40,128]{3,2,1,0:T(8,128)S(1)}, f32[4,128]{1,0:T(4,128)S(1)}, f32[4,128]{1,0:T(4,128)S(1)}, f32[8,128]{1,0:T(8,128)S(1)}) custom-call(f32[24,128]{1,0:T(8,128)S(1)} %get-tuple-element.32.wl_ref, f32[5,8,9,8,128]{4,3,2,1,0:T(8,128)} %shard_map.98.y_hbm, f32[4,9,48,128]{3,2,1,0:T(8,128)S(1)} %get-tuple-element.34.stat_ref, ...), custom_call_target="tpu_custom_call" | custom-call | flops 4000000 | bytes 4000000 | tf_op jit(solution)/shard_map/pallas_call | solution.py:490
  116.3 0.1 collective-permute-start.5
  116.5 1.1 collective-permute-done.5
  117.6 0.6 broadcast_in_dim.15
  118.2 5.6 %all-to-all-start.2 = ((f32[32,4,128]{2,1,0:T(4,128)}), f32[32,4,128]{2,1,0:T(4,128)S(1)}, u32[]{:S(2)}, u32[]{:S(2)}) async-start(f32[32,4,128]{2,1,0:T(4,128)} %broadcast_in_dim.15), calls=%async_computation.2 | async-start | bytes 131072 | tf_op jit(solution)/shard_map/all_to_all | solution.py:535
  123.9 7.6 %shard_map.100.y_hbm = f32[4,8,9,8,128]{4,3,2,1,0:T(8,128)} custom-call(f32[7,7]{1,0:T(8,128)S(1)} %copy-done.1, f32[5,9,40,128]{3,2,1,0:T(8,128)S(1)} %get-tuple-element.43.dyn_in, f32[8,48,128]{2,1,0:T(8,128)S(1)} %get-tuple-element.38.r_ref, f32[48,128]{1,0:T(8,128)S(1)} %get-tuple-element.39.r8_ref), custom_call_target="tpu_custom_call" | custom-call | flops 40000000 | bytes 40000000 | tf_op jit(solution)/shard_map/pallas_call | solution.py:490
  131.5 18.0 %all-to-all-done.2 = f32[32,4,128]{2,1,0:T(4,128)S(1)} async-done(((f32[32,4,128]{2,1,0:T(4,128)}), f32[32,4,128]{2,1,0:T(4,128)S(1)}, u32[]{:S(2)}, u32[]{:S(2)}) %all-to-all-start.2) | async-done | bytes 65568 | tf_op jit(solution)/shard_map/all_to_all | solution.py:535
  149.4 2.7 %shard_map.101 = (f32[3,32,1080]{2,1,0:T(8,128)}, f32[32,1080]{1,0:T(8,128)}, f32[3]{0:T(128)}) custom-call(f32[24,128]{1,0:T(8,128)S(1)} %get-tuple-element.32.wl_ref, f32[4,8,9,8,128]{4,3,2,1,0:T(8,128)} %shard_map.100.y_hbm, f32[48,128]{1,0:T(8,128)S(1)} %get-tuple-element.39.r8_ref, f32[128,128]{1,0:T(8,128)S(1)} %bitcast.6, ...), custom_call_target="tpu_custom_call" | custom-call | flops 4000000 | bytes 4000000 | tf_op jit(solution)/shard_map/pallas_call | solution.py:490
  (5 shorter events, 0.0 us)
Async XLA Ops:
  0.6 39.6 %copy-start = (s32[1024]{0:T(1024)S(1)}, s32[1024]{0:T(1024)}, u32[]{:S(2)}) copy-start(s32[1024]{0:T(1024)} %param.12) | copy-start | bytes 12292
  2.4 51.6 %copy-start.1 = (f32[7,7]{1,0:T(8,128)S(1)}, f32[7,7]{1,0:T(8,128)}, u32[]{:S(2)}) copy-start(f32[7,7]{1,0:T(8,128)} %w_ref.5) | copy-start | bytes 592
  2.5 1.5 collective-permute-start
  2.6 1.3 collective-permute-start.1
  4.6 61.9 %all-to-all-start = ((f32[32,4,128]{2,1,0:T(4,128)}), f32[32,4,128]{2,1,0:T(4,128)S(1)}, u32[]{:S(2)}, u32[]{:S(2)}) async-start(f32[32,4,128]{2,1,0:T(4,128)} %get-tuple-element.36), calls=%async_computation | async-start | bytes 131072 | tf_op jit(solution)/shard_map/all_to_all | solution.py:516
  37.3 14.5 %collective-permute-start.2 = (f32[9,9,8,128]{3,2,1,0:T(8,128)S(1)}, f32[9,9,8,128]{3,2,1,0:T(8,128)S(1)}, u32[]{:S(2)}, u32[]{:S(2)}) collective-permute-start(f32[9,9,8,128]{3,2,1,0:T(8,128)S(1)} %get-tuple-element.30), channel_id=1, source_target_pairs={{2,0},{4,2},{6,4},{8,6},{10,8},{12,10},{14,12},{16,14},{18,16},{20... | collective-permute-start | bytes 995336 | tf_op jit(solution)/shard_map/ppermute | solution.py:515
  40.2 13.9 %collective-permute-start.3 = (f32[9,9,8,128]{3,2,1,0:T(8,128)S(1)}, f32[9,9,8,128]{3,2,1,0:T(8,128)S(1)}, u32[]{:S(2)}, u32[]{:S(2)}) collective-permute-start(f32[9,9,8,128]{3,2,1,0:T(8,128)S(1)} %get-tuple-element.31), channel_id=1, source_target_pairs={{0,2},{2,4},{4,6},{6,8},{8,10},{10,12},{12,14},{14,16},{16,18},{18... | collective-permute-start | bytes 995336 | tf_op jit(solution)/shard_map/ppermute | solution.py:514
  68.3 1.3 collective-permute-start.4
  70.2 44.5 %all-to-all-start.1 = ((f32[32,4,128]{2,1,0:T(4,128)}), f32[32,4,128]{2,1,0:T(4,128)S(1)}, u32[]{:S(2)}, u32[]{:S(2)}) async-start(f32[32,4,128]{2,1,0:T(4,128)} %broadcast_in_dim.14), calls=%async_computation.1 | async-start | bytes 131072 | tf_op jit(solution)/shard_map/all_to_all | solution.py:535
  116.3 1.3 collective-permute-start.5
  118.2 31.2 %all-to-all-start.2 = ((f32[32,4,128]{2,1,0:T(4,128)}), f32[32,4,128]{2,1,0:T(4,128)S(1)}, u32[]{:S(2)}, u32[]{:S(2)}) async-start(f32[32,4,128]{2,1,0:T(4,128)} %broadcast_in_dim.15), calls=%async_computation.2 | async-start | bytes 131072 | tf_op jit(solution)/shard_map/all_to_all | solution.py:535
